TPU v7x, 512 devices: a whole 4x8x8 slice. The times are simulated.
512 devices in a mesh: mem: 16 (over z_lo, y), tile: 32 (over z_hi, x, core).
Axes of the slice: x: 4, y: 8, z: 8 (z_hi: 4, z_lo: 2; z = z_hi * 2 + z_lo), core: 2. Of those that a mesh axis runs over, the one named last changes fastest.
Arguments:
- perturbations: bfloat16 [384, 3, 32, 32768], P('mem', None, None, 'tile'), may hold values from -6 to 6
- member_weight: float32 [384], P('mem'), may hold values from 0.3 to 3
- innovation: float32 [3, 32, 32768], P(None, 'mem', 'tile'), may hold values from -6 to 6
- obs_weight: float32 [3, 32], P(None, 'mem'), may hold values from 0.1 to 1
- static_var: float32 [3, 32, 32768], P(None, 'mem', 'tile'), may hold values from 0.1 to 1
- obs_mask: int32 [32768], P('tile'), may hold values 0 or 1
- kernel_x: float32 [32, 5], replicated, may hold values from 0.1 to 0.5
- kernel_y: float32 [32, 5], replicated, may hold values from 0.1 to 0.5
Outputs:
- analysis: float32 [3, 32, 32768], P(None, 'mem', 'tile')
All inputs are finite; a program needn't handle non-finite values. No bound on the sum of `obs_mask` on one device may be relied on, other than what follows from the above.
Results may differ from a plain program's by a relative error of at most 0.0003.
Values sent between devices are 32-bit elements; how exact they have to be, the bound alone decides.
No kernel may reach another device: no remote copies, remote signals or barrier semaphores. Data moves between devices by JAX's collectives and lax.ppermute only.
A program may use at most 64 MiB of HBM per device.

v0:
```python
import functools
import math

import jax
import jax.numpy as jnp
import numpy as np
from jax import lax
from jax.experimental import pallas as pl
from jax.experimental.pallas import tpu as pltpu
from jax.sharding import PartitionSpec as P

VARS = 3
TILE_X = 32
TILE_Y = 32
GRID_Y = 4
STEPS = 2
CX = TILE_X // 2
CY = TILE_Y // 2
CELLS = CX * CY
COLS = TILE_X * TILE_Y
LANES = 128
CB = COLS // LANES
ROWS = VARS * CB
EXT = CX + 8
F32 = jnp.float32
BF16 = jnp.bfloat16


def interp_rows(fine_count):
    coarse_count = fine_count // 2
    rows = np.zeros((fine_count, coarse_count), np.float32)
    for i in range(fine_count):
        upper = 0.75 if i % 2 == 0 else 0.25
        low = (i - 1) // 2
        rows[i, min(max(low, 0), coarse_count - 1)] += 1.0 - upper
        rows[i, min(max(low + 1, 0), coarse_count - 1)] += upper
    return rows


def interp_matrix():
    rows_x, rows_y = interp_rows(TILE_X), interp_rows(TILE_Y)
    full = np.einsum("ia,jb->baij", rows_x, rows_y)
    return full.reshape(CELLS, COLS)


def vmem():
    return pl.BlockSpec(memory_space=pltpu.VMEM)


def grant(mib):
    return pltpu.CompilerParams(vmem_limit_bytes=mib * 1024 * 1024)


def split_terms(x):
    high = x.astype(BF16)
    return high, (x - high.astype(F32)).astype(BF16)


def split_levels_kernel(p_ref, _, o_ref, s_ref, *, own):
    members, _, levels, _ = p_ref.shape
    owners = levels // own
    start = pl.program_id(0) * members

    def one(k, carry):
        for v in range(VARS):
            for c in range(CB):
                s_ref[v * CB + c] = p_ref[k, v, :, c * LANES : (c + 1) * LANES].astype(F32)
        for v in range(VARS):
            for c in range(CB):
                for q in range(own):
                    o_ref[start + k, v, q, c] = s_ref[v * CB + c, pl.ds(q, owners, stride=own), :]
        return carry

    lax.fori_loop(0, members, one, 0)


def split_levels(perturbations, after, own):
    members, _, levels, _ = perturbations.shape
    step = math.gcd(members, 4)
    return pl.pallas_call(
        functools.partial(split_levels_kernel, own=own),
        grid=(members // step,),
        in_specs=[
            pl.BlockSpec((step, VARS, levels, COLS), lambda k: (k, 0, 0, 0)),
            pl.BlockSpec(memory_space=pl.ANY),
        ],
        out_specs=vmem(),
        out_shape=jax.ShapeDtypeStruct((members, VARS, own, CB, levels // own, LANES), F32),
        scratch_shapes=[pltpu.VMEM((VARS * CB, levels, LANES), F32)],
        compiler_params=grant(6),
        cost_estimate=pl.CostEstimate(flops=400_000_000, bytes_accessed=10_000_000, transcendentals=0),
        name="split_levels",
    )(perturbations, after)


def project_kernel(p_ref, g_ref, m_ref, c_ref, ylo_ref, yhi_ref, hi_ref, lo_ref, *, chunks):
    members, _, _, _, owners, _ = p_ref.shape
    tiles = members * owners // LANES
    for n, q in enumerate(chunks):
        for c in range(CB):
            lanes = slice(c * LANES, (c + 1) * LANES)
            grad = [
                g_ref[pl.ds((n * VARS + v) * CB + c, owners, stride=len(chunks) * ROWS), :]
                for v in range(VARS)
            ]

            def one(k, carry):
                acc = p_ref[k, 0, q, c] * grad[0]
                for v in range(1, VARS):
                    acc = acc + p_ref[k, v, q, c] * grad[v]
                high, low = split_terms(acc)
                at = pl.ds(pl.multiple_of(k * owners, owners), owners)
                hi_ref[at, lanes] = high
                lo_ref[at, lanes] = low
                return carry

            lax.fori_loop(0, members, one, 0, unroll=4)
        dims = (((1,), (1,)), ((), ()))
        coarse = lax.dot_general(m_ref[...], hi_ref[...], dims, preferred_element_type=F32)
        coarse = coarse + lax.dot_general(m_ref[...], lo_ref[...], dims, preferred_element_type=F32)
        for t in range(tiles):
            piece = coarse[:, t * LANES : (t + 1) * LANES]
            c_ref[n * tiles + t] = piece
            ylo_ref[n * tiles + t] = piece[: 2 * CX]
            yhi_ref[n * tiles + t] = piece[CELLS - 2 * CX :]


def project(split, gathered, matrix, chunks):
    members, _, _, _, owners, _ = split.shape
    tiles = len(chunks) * members * owners // LANES
    return pl.pallas_call(
        functools.partial(project_kernel, chunks=chunks),
        in_specs=[vmem(), vmem(), vmem()],
        out_specs=[vmem(), vmem(), vmem()],
        out_shape=[
            jax.ShapeDtypeStruct((tiles, CELLS, LANES), F32),
            jax.ShapeDtypeStruct((tiles, 2 * CX, LANES), F32),
            jax.ShapeDtypeStruct((tiles, 2 * CX, LANES), F32),
        ],
        scratch_shapes=[
            pltpu.VMEM((members * owners, COLS), BF16),
            pltpu.VMEM((members * owners, COLS), BF16),
        ],
        compiler_params=grant(8),
        name="project",
    )(split, gathered, matrix)


def smooth_y_kernel(c_ref, prev_ref, next_ref, k_ref, s_ref, xlo_ref, xhi_ref, *, chunks):
    tiles = c_ref.shape[0]
    for t in range(tiles):
        q = chunks[t * len(chunks) // tiles]
        coef = [k_ref[d : d + 1, q * LANES : (q + 1) * LANES] for d in range(5)]

        def rows(b):
            if b < 0:
                return prev_ref[t, (b + 2) * CX : (b + 3) * CX, :]
            if b >= CY:
                return next_ref[t, (b - CY) * CX : (b - CY + 1) * CX, :]
            return c_ref[t, b * CX : (b + 1) * CX, :]

        for b in range(CY):
            acc = coef[0] * rows(b - 2)
            for d in range(1, 5):
                acc = acc + coef[d] * rows(b + d - 2)
            s_ref[t, b * CX : (b + 1) * CX, :] = acc
        for j in range(2):
            xlo_ref[t, j * CY : (j + 1) * CY, :] = s_ref[t, pl.ds(j, CY, stride=CX), :]
            xhi_ref[t, j * CY : (j + 1) * CY, :] = s_ref[t, pl.ds(CX - 2 + j, CY, stride=CX), :]


def smooth_y(coarse, from_prev, from_next, coefs, chunks):
    tiles = coarse.shape[0]
    return pl.pallas_call(
        functools.partial(smooth_y_kernel, chunks=chunks),
        in_specs=[vmem()] * 4,
        out_specs=[vmem()] * 3,
        out_shape=[
            jax.ShapeDtypeStruct((tiles, CELLS, LANES), F32),
            jax.ShapeDtypeStruct((tiles, 2 * CY, LANES), F32),
            jax.ShapeDtypeStruct((tiles, 2 * CY, LANES), F32),
        ],
        compiler_params=grant(2),
        name="smooth_y",
    )(coarse, from_prev, from_next, coefs)


def increment_kernel(p_ref, s_ref, prev_ref, next_ref, k_ref, w_ref, m_ref, o_ref, e_ref, hi_ref, lo_ref, f_ref, *, chunks):
    members, _, _, _, owners, _ = p_ref.shape
    tiles = members * owners // LANES
    for n, q in enumerate(chunks):
        for t in range(tiles):
            at = n * tiles + t
            for b in range(CY):
                e_ref[b * EXT + 8 : b * EXT + 8 + CX, :] = s_ref[at, b * CX : (b + 1) * CX, :]
            for j in range(2):
                e_ref[pl.ds(6 + j, CY, stride=EXT), :] = prev_ref[at, j * CY : (j + 1) * CY, :]
                e_ref[pl.ds(8 + CX + j, CY, stride=EXT), :] = next_ref[at, j * CY : (j + 1) * CY, :]
            scale = w_ref[:, t * LANES : (t + 1) * LANES]
            coef = [k_ref[d : d + 1, q * LANES : (q + 1) * LANES] * scale for d in range(5)]
            for b in range(CY):
                acc = coef[0] * e_ref[b * EXT + 6 : b * EXT + 6 + CX, :]
                for d in range(1, 5):
                    acc = acc + coef[d] * e_ref[b * EXT + 6 + d : b * EXT + 6 + d + CX, :]
                high, low = split_terms(acc)
                hi_ref[b * CX : (b + 1) * CX, t * LANES : (t + 1) * LANES] = high
                lo_ref[b * CX : (b + 1) * CX, t * LANES : (t + 1) * LANES] = low
        dims = (((0,), (0,)), ((), ()))
        fine = lax.dot_general(hi_ref[...], m_ref[...], dims, preferred_element_type=F32)
        f_ref[...] = fine + lax.dot_general(lo_ref[...], m_ref[...], dims, preferred_element_type=F32)
        for c in range(CB):
            lanes = slice(c * LANES, (c + 1) * LANES)

            def one(k, acc):
                at = pl.ds(pl.multiple_of(k * owners, owners), owners)
                local = f_ref[at, lanes]
                return tuple(acc[v] + p_ref[k, v, q, c] * local for v in range(VARS))

            zero = jnp.zeros((owners, LANES), F32)
            acc = lax.fori_loop(0, members, one, (zero,) * VARS, unroll=4)
            for v in range(VARS):
                o_ref[pl.ds((n * VARS + v) * CB + c, owners, stride=len(chunks) * ROWS), :] = acc[v]


def increment(split, smoothed, from_prev, from_next, coefs, scale, matrix, chunks):
    members, _, _, _, owners, _ = split.shape
    return pl.pallas_call(
        functools.partial(increment_kernel, chunks=chunks),
        in_specs=[vmem()] * 7,
        out_specs=vmem(),
        out_shape=jax.ShapeDtypeStruct((owners * len(chunks) * ROWS, LANES), F32),
        scratch_shapes=[
            pltpu.VMEM((CY * EXT + 8, LANES), F32),
            pltpu.VMEM((CELLS, members * owners), BF16),
            pltpu.VMEM((CELLS, members * owners), BF16),
            pltpu.VMEM((members * owners, COLS), F32),
        ],
        compiler_params=grant(8),
        name="increment",
    )(split, smoothed, from_prev, from_next, coefs, scale, matrix)


def prepare_kernel(
    inn_ref, sv_ref, mask_ref, w_ref, kx_ref, ky_ref, mw_ref, level_ref, member_ref,
    innov_ref, static_ref, weight_ref, grad_ref, send_ref, cx_ref, cy_ref, scale_ref,
    *, norm,
):
    own = inn_ref.shape[1]
    for q in range(own):
        for v in range(VARS):
            for c in range(CB):
                row = (q * VARS + v) * CB + c
                lanes = slice(c * LANES, (c + 1) * LANES)
                innov_ref[row : row + 1, :] = inn_ref[v, q : q + 1, lanes]
                static_ref[row : row + 1, :] = sv_ref[v, q : q + 1, lanes]
            rows = slice((q * VARS + v) * CB, (q * VARS + v + 1) * CB)
            weight_ref[rows, :] = mask_ref[...].astype(F32) * w_ref[v, q]
    grad = weight_ref[...] * (0.0 - innov_ref[...])
    grad_ref[...] = grad
    rows = grad.shape[0]
    for d in range(send_ref.shape[0] // rows):
        send_ref[d * rows : (d + 1) * rows, :] = grad
    exact = lax.Precision.HIGHEST
    cx_ref[...] = jnp.dot(kx_ref[...], level_ref[...], precision=exact, preferred_element_type=F32)
    cy_ref[...] = jnp.dot(ky_ref[...], level_ref[...], precision=exact, preferred_element_type=F32)
    scale = jnp.dot(mw_ref[...], member_ref[...], precision=exact, preferred_element_type=F32)
    scale_ref[...] = scale / norm


def prepare(innovation, static_var, obs_mask, obs_weight, kernel_x, kernel_y, member_weight, size):
    _, own, _ = innovation.shape
    members, levels = member_weight.shape[0], kernel_x.shape[0]
    rows = own * ROWS
    lane = np.arange(own * LANES)
    level = own * (lane % LANES % size) + lane // LANES
    pick_level = (np.arange(levels)[:, None] == level[None, :]).astype(np.float32)
    pick_member = (np.arange(members)[:, None] == np.arange(members * size)[None, :] // size).astype(np.float32)
    flat = [jax.ShapeDtypeStruct((rows, LANES), F32)] * 4
    coefs = [jax.ShapeDtypeStruct((5, own * LANES), F32)] * 2
    return pl.pallas_call(
        functools.partial(prepare_kernel, norm=float(size * members)),
        in_specs=[vmem()] * 3 + [pl.BlockSpec(memory_space=pltpu.SMEM)] + [vmem()] * 5,
        out_specs=[vmem()] * 8,
        out_shape=flat
        + [jax.ShapeDtypeStruct((size * rows, LANES), F32)]
        + coefs
        + [jax.ShapeDtypeStruct((1, members * size), F32)],
        compiler_params=grant(2),
        name="prepare",
    )(
        innovation, static_var, obs_mask.reshape(CB, LANES), obs_weight, kernel_x.T, kernel_y.T,
        member_weight.reshape(1, -1), jnp.asarray(pick_level), jnp.asarray(pick_member),
    )


def update_kernel(r_ref, *refs, size, last):
    ins, outs = (refs[:3], refs[3:]) if last else (refs[:4], refs[4:])
    rows = ins[0].shape[0]
    total = r_ref[:rows, :]
    for d in range(1, size):
        total = total + r_ref[d * rows : (d + 1) * rows, :]
    if last:
        a_ref, g_ref, sv_ref = ins
        analysis = a_ref[...]
    else:
        g_ref, sv_ref, w_ref, inn_ref = ins
        analysis = jnp.zeros_like(total)
    inc = total + sv_ref[...] * g_ref[...]
    analysis = analysis - 0.5 * (analysis + inc)
    if last:
        own = rows // ROWS
        for q in range(own):
            for v in range(VARS):
                for c in range(CB):
                    row = (q * VARS + v) * CB + c
                    outs[0][v, q : q + 1, c * LANES : (c + 1) * LANES] = analysis[row : row + 1, :]
        return
    grad = w_ref[...] * (analysis - inn_ref[...])
    outs[0][...] = analysis
    outs[1][...] = grad
    for d in range(size):
        outs[2][d * rows : (d + 1) * rows, :] = grad


def update(received, args, size, last):
    rows = received.shape[0] // size
    flat = jax.ShapeDtypeStruct((rows, LANES), F32)
    if last:
        shapes = [jax.ShapeDtypeStruct((VARS, rows // ROWS, COLS), F32)]
    else:
        shapes = [flat, flat, jax.ShapeDtypeStruct((size * rows, LANES), F32)]
    return pl.pallas_call(
        functools.partial(update_kernel, size=size, last=last),
        in_specs=[vmem()] * (1 + len(args)),
        out_specs=[vmem()] * len(shapes),
        out_shape=shapes,
        compiler_params=grant(2),
        name="update",
    )(received, *args)


def exchange(x, size):
    blocks = x.reshape(size, -1, LANES)
    return lax.all_to_all(blocks, "mem", 0, 0, tiled=True).reshape(x.shape)


def along_x(x, by):
    size = lax.axis_size("tile")
    return lax.ppermute(x, "tile", [(i, (i + by * GRID_Y) % size) for i in range(size)])


def along_y(x, by):
    size = lax.axis_size("tile")
    return lax.ppermute(x, "tile", [(i, i + by) for i in range(size) if 0 <= i % GRID_Y + by < GRID_Y])


def body(perturbations, member_weight, innovation, obs_weight, static_var, obs_mask, kernel_x, kernel_y):
    size = lax.axis_size("mem")
    own = perturbations.shape[2] // size
    chunks = tuple(range(own))
    matrix = jnp.asarray(interp_matrix(), BF16)
    innov, static, weight, gradient, to_send, coef_x, coef_y, scale = prepare(
        innovation, static_var, obs_mask, obs_weight, kernel_x, kernel_y, member_weight, size
    )
    analysis = split = None
    for step in range(STEPS):
        gathered = exchange(to_send, size)
        if split is None:
            split = split_levels(perturbations, gathered, own)
        coarse, ylo, yhi = project(split, gathered, matrix, chunks)
        from_prev, from_next = along_y(yhi, 1), along_y(ylo, -1)
        smoothed, xlo, xhi = smooth_y(coarse, from_prev, from_next, coef_y, chunks)
        from_prev, from_next = along_x(xhi, 1), along_x(xlo, -1)
        partial = increment(split, smoothed, from_prev, from_next, coef_x, scale, matrix, chunks)
        received = exchange(partial, size)
        if step == STEPS - 1:
            return update(received, (analysis, gradient, static), size, True)[0]
        analysis, gradient, to_send = update(received, (gradient, static, weight, innov), size, False)


def solution(mesh):
    placed = (
        P("mem", None, None, "tile"),
        P("mem"),
        P(None, "mem", "tile"),
        P(None, "mem"),
        P(None, "mem", "tile"),
        P("tile"),
        P(),
        P(),
    )
    return jax.shard_map(
        body, mesh=mesh, in_specs=placed, out_specs=P(None, "mem", "tile"), check_vma=False
    )
```

profile of v0, /device:TPU:12, one launch (start us, length us, event | category | flops | bytes accessed | tf_op | source)
XLA Modules:
  0.0 146.0 jit_solution(8291455338116338561)
XLA Ops:
  0.0 0.8 copy.12.w_ref
  6.5 0.8 prepare.1
  7.3 21.6 %all_to_all.20 = f32[16,48,128]{2,1,0:T(8,128)S(1)} all-to-all(f32[16,48,128]{2,1,0:T(8,128)S(1)} %bitcast.19), channel_id=1, replica_groups=mesh['mem'=16,'tile'=32] {'mem'}, dimensions={0} | all-to-all | bytes 786432 | tf_op jit(solution)/shard_map/all_to_all | solution.py:344
  28.9 2.3 %copy-done.1 = bf16[24,3,32,1024]{3,2,1,0:T(8,128)(2,1)S(1)} copy-done((bf16[24,3,32,1024]{3,2,1,0:T(8,128)(2,1)S(1)}, bf16[24,3,32,1024]{3,2,1,0:T(8,128)(2,1)}, u32[]{:S(2)}) %copy-start.1) | copy-done | bytes 4718616
  31.3 1.4 split_levels.1.p_ref
  32.7 3.3 %project.2 = (f32[6,256,128]{2,1,0:T(8,128)S(1)}, f32[6,32,128]{2,1,0:T(8,128)S(1)}, f32[6,32,128]{2,1,0:T(8,128)S(1)}) custom-call(f32[24,3,2,8,16,128]{5,4,3,2,1,0:T(8,128)S(1)} %split_levels.1.p_ref, f32[768,128]{1,0:T(8,128)S(1)} %bitcast.13, bf16[256,1024]{1,0:T(8,128)(2,1)S(1)} %copy-done), custom_call_target="tpu_custom_call" | custom-call | tf_op jit(solution)/shard_map/project/pallas_call | solution.py:131
  35.9 1.3 collective-permute-start
  37.2 1.3 collective-permute-start.1
  38.5 3.3 %collective-permute-done.1.next_ref = f32[6,32,128]{2,1,0:T(8,128)S(1)} collective-permute-done((f32[6,32,128]{2,1,0:T(8,128)S(1)}, f32[6,32,128]{2,1,0:T(8,128)S(1)}, u32[]{:S(2)}, u32[]{:S(2)}) %collective-permute-start.1) | collective-permute-done | bytes 98336 | tf_op jit(solution)/shard_map/ppermute | solution.py:354
  42.1 6.3 %collective-permute-start.2 = (f32[6,32,128]{2,1,0:T(8,128)S(1)}, f32[6,32,128]{2,1,0:T(8,128)S(1)}, u32[]{:S(2)}, u32[]{:S(2)}) collective-permute-start(f32[6,32,128]{2,1,0:T(8,128)S(1)} %get-tuple-element.34), channel_id=1, source_target_pairs={{0,4},{1,5},{2,6},{3,7},{4,8},{5,9},{6,10},{7,11},{8,12},{9,13},{1... | collective-permute-start | bytes 294920 | tf_op jit(solution)/shard_map/ppermute | solution.py:349
  48.5 1.9 %collective-permute-start.3 = (f32[6,32,128]{2,1,0:T(8,128)S(1)}, f32[6,32,128]{2,1,0:T(8,128)S(1)}, u32[]{:S(2)}, u32[]{:S(2)}) collective-permute-start(f32[6,32,128]{2,1,0:T(8,128)S(1)} %get-tuple-element.35), channel_id=1, source_target_pairs={{0,28},{1,29},{2,30},{3,31},{4,0},{5,1},{6,2},{7,3},{8,4},{9,5},{1... | collective-permute-start | bytes 294920 | tf_op jit(solution)/shard_map/ppermute | solution.py:349
  50.7 7.6 %collective-permute-done.3.next_ref = f32[6,32,128]{2,1,0:T(8,128)S(1)} collective-permute-done((f32[6,32,128]{2,1,0:T(8,128)S(1)}, f32[6,32,128]{2,1,0:T(8,128)S(1)}, u32[]{:S(2)}, u32[]{:S(2)}) %collective-permute-start.3) | collective-permute-done | bytes 98336 | tf_op jit(solution)/shard_map/ppermute | solution.py:349
  58.3 3.0 %increment.2 = f32[768,128]{1,0:T(8,128)S(1)} custom-call(f32[24,3,2,8,16,128]{5,4,3,2,1,0:T(8,128)S(1)} %split_levels.1.p_ref, f32[6,256,128]{2,1,0:T(8,128)S(1)} %get-tuple-element.33.s_ref, f32[6,32,128]{2,1,0:T(8,128)S(1)} %collective-permute-done.2.prev_ref, f32[6,32,128]{2,1,0:T(8,128)S(1)} %collective-permute-done.3.next_ref, ...), custom_call_target="tpu_custom_call" | custom-call | tf_op jit(solution)/shard_map/increment/pallas_call | solution.py:227
  61.3 20.6 %all_to_all.21 = f32[16,48,128]{2,1,0:T(8,128)S(1)} all-to-all(f32[16,48,128]{2,1,0:T(8,128)S(1)} %bitcast.18), channel_id=1, replica_groups=mesh['mem'=16,'tile'=32] {'mem'}, dimensions={0} | all-to-all | bytes 786432 | tf_op jit(solution)/shard_map/all_to_all | solution.py:344
  81.9 17.1 %all_to_all.22 = f32[16,48,128]{2,1,0:T(8,128)S(1)} all-to-all(f32[16,48,128]{2,1,0:T(8,128)S(1)} %bitcast.20), channel_id=1, replica_groups=mesh['mem'=16,'tile'=32] {'mem'}, dimensions={0} | all-to-all | bytes 786432 | tf_op jit(solution)/shard_map/all_to_all | solution.py:344
  99.0 3.3 %project.3 = (f32[6,256,128]{2,1,0:T(8,128)S(1)}, f32[6,32,128]{2,1,0:T(8,128)S(1)}, f32[6,32,128]{2,1,0:T(8,128)S(1)}) custom-call(f32[24,3,2,8,16,128]{5,4,3,2,1,0:T(8,128)S(1)} %split_levels.1.p_ref, f32[768,128]{1,0:T(8,128)S(1)} %bitcast.14, bf16[256,1024]{1,0:T(8,128)(2,1)S(1)} %copy-done), custom_call_target="tpu_custom_call" | custom-call | tf_op jit(solution)/shard_map/project/pallas_call | solution.py:131
  102.3 1.3 collective-permute-start.4
  103.6 1.3 collective-permute-start.5
  104.9 1.9 %collective-permute-done.5.next_ref = f32[6,32,128]{2,1,0:T(8,128)S(1)} collective-permute-done((f32[6,32,128]{2,1,0:T(8,128)S(1)}, f32[6,32,128]{2,1,0:T(8,128)S(1)}, u32[]{:S(2)}, u32[]{:S(2)}) %collective-permute-start.5) | collective-permute-done | bytes 98336 | tf_op jit(solution)/shard_map/ppermute | solution.py:354
  107.0 2.9 %collective-permute-start.6 = (f32[6,32,128]{2,1,0:T(8,128)S(1)}, f32[6,32,128]{2,1,0:T(8,128)S(1)}, u32[]{:S(2)}, u32[]{:S(2)}) collective-permute-start(f32[6,32,128]{2,1,0:T(8,128)S(1)} %get-tuple-element.47), channel_id=1, source_target_pairs={{0,4},{1,5},{2,6},{3,7},{4,8},{5,9},{6,10},{7,11},{8,12},{9,13},{1... | collective-permute-start | bytes 294920 | tf_op jit(solution)/shard_map/ppermute | solution.py:349
  110.0 4.4 %collective-permute-start.7 = (f32[6,32,128]{2,1,0:T(8,128)S(1)}, f32[6,32,128]{2,1,0:T(8,128)S(1)}, u32[]{:S(2)}, u32[]{:S(2)}) collective-permute-start(f32[6,32,128]{2,1,0:T(8,128)S(1)} %get-tuple-element.48), channel_id=1, source_target_pairs={{0,28},{1,29},{2,30},{3,31},{4,0},{5,1},{6,2},{7,3},{8,4},{9,5},{1... | collective-permute-start | bytes 294920 | tf_op jit(solution)/shard_map/ppermute | solution.py:349
  115.1 7.2 %collective-permute-done.7.next_ref = f32[6,32,128]{2,1,0:T(8,128)S(1)} collective-permute-done((f32[6,32,128]{2,1,0:T(8,128)S(1)}, f32[6,32,128]{2,1,0:T(8,128)S(1)}, u32[]{:S(2)}, u32[]{:S(2)}) %collective-permute-start.7) | collective-permute-done | bytes 98336 | tf_op jit(solution)/shard_map/ppermute | solution.py:349
  122.2 3.0 %increment.3 = f32[768,128]{1,0:T(8,128)S(1)} custom-call(f32[24,3,2,8,16,128]{5,4,3,2,1,0:T(8,128)S(1)} %split_levels.1.p_ref, f32[6,256,128]{2,1,0:T(8,128)S(1)} %get-tuple-element.46.s_ref, f32[6,32,128]{2,1,0:T(8,128)S(1)} %collective-permute-done.6.prev_ref, f32[6,32,128]{2,1,0:T(8,128)S(1)} %collective-permute-done.7.next_ref, ...), custom_call_target="tpu_custom_call" | custom-call | tf_op jit(solution)/shard_map/increment/pallas_call | solution.py:227
  125.2 20.1 %all_to_all.23 = f32[16,48,128]{2,1,0:T(8,128)S(1)} all-to-all(f32[16,48,128]{2,1,0:T(8,128)S(1)} %bitcast.17), channel_id=1, replica_groups=mesh['mem'=16,'tile'=32] {'mem'}, dimensions={0} | all-to-all | bytes 786432 | tf_op jit(solution)/shard_map/all_to_all | solution.py:344
  (27 shorter events, 7.9 us)
Async XLA Ops:
  0.0 32.7 %copy-start = (bf16[256,1024]{1,0:T(8,128)(2,1)S(1)}, bf16[256,1024]{1,0:T(8,128)(2,1)}, u32[]{:S(2)}) copy-start(bf16[256,1024]{1,0:T(8,128)(2,1)} %constant.6.clone.m_ref) | copy-start | bytes 1572868
  0.8 0.8 copy-start.2
  1.6 0.8 copy-start.3
  2.4 0.7 copy-start.4
  3.1 0.7 copy-start.5
  3.8 0.7 copy-start.6
  4.5 0.7 copy-start.7
  5.2 0.7 copy-start.8
  5.9 0.7 copy-start.9
  28.9 2.3 %copy-start.1 = (bf16[24,3,32,1024]{3,2,1,0:T(8,128)(2,1)S(1)}, bf16[24,3,32,1024]{3,2,1,0:T(8,128)(2,1)}, u32[]{:S(2)}) copy-start(bf16[24,3,32,1024]{3,2,1,0:T(8,128)(2,1)} %p_ref.1) | copy-start | bytes 14155780
  35.9 2.6 %collective-permute-start = (f32[6,32,128]{2,1,0:T(8,128)S(1)}, f32[6,32,128]{2,1,0:T(8,128)S(1)}, u32[]{:S(2)}, u32[]{:S(2)}) collective-permute-start(f32[6,32,128]{2,1,0:T(8,128)S(1)} %get-tuple-element.30), channel_id=1, source_target_pairs={{0,1},{1,2},{2,3},{4,5},{5,6},{6,7},{8,9},{9,10},{10,11},{12,13},{... | collective-permute-start | bytes 294920 | tf_op jit(solution)/shard_map/ppermute | solution.py:354
  37.2 4.6 %collective-permute-start.1 = (f32[6,32,128]{2,1,0:T(8,128)S(1)}, f32[6,32,128]{2,1,0:T(8,128)S(1)}, u32[]{:S(2)}, u32[]{:S(2)}) collective-permute-start(f32[6,32,128]{2,1,0:T(8,128)S(1)} %get-tuple-element.31), channel_id=1, source_target_pairs={{1,0},{2,1},{3,2},{5,4},{6,5},{7,6},{9,8},{10,9},{11,10},{13,12},{... | collective-permute-start | bytes 294920 | tf_op jit(solution)/shard_map/ppermute | solution.py:354
  42.1 8.5 %collective-permute-start.2 = (f32[6,32,128]{2,1,0:T(8,128)S(1)}, f32[6,32,128]{2,1,0:T(8,128)S(1)}, u32[]{:S(2)}, u32[]{:S(2)}) collective-permute-start(f32[6,32,128]{2,1,0:T(8,128)S(1)} %get-tuple-element.34), channel_id=1, source_target_pairs={{0,4},{1,5},{2,6},{3,7},{4,8},{5,9},{6,10},{7,11},{8,12},{9,13},{1... | collective-permute-start | bytes 294920 | tf_op jit(solution)/shard_map/ppermute | solution.py:349
  48.5 9.8 %collective-permute-start.3 = (f32[6,32,128]{2,1,0:T(8,128)S(1)}, f32[6,32,128]{2,1,0:T(8,128)S(1)}, u32[]{:S(2)}, u32[]{:S(2)}) collective-permute-start(f32[6,32,128]{2,1,0:T(8,128)S(1)} %get-tuple-element.35), channel_id=1, source_target_pairs={{0,28},{1,29},{2,30},{3,31},{4,0},{5,1},{6,2},{7,3},{8,4},{9,5},{1... | collective-permute-start | bytes 294920 | tf_op jit(solution)/shard_map/ppermute | solution.py:349
  102.3 2.6 %collective-permute-start.4 = (f32[6,32,128]{2,1,0:T(8,128)S(1)}, f32[6,32,128]{2,1,0:T(8,128)S(1)}, u32[]{:S(2)}, u32[]{:S(2)}) collective-permute-start(f32[6,32,128]{2,1,0:T(8,128)S(1)} %get-tuple-element.44), channel_id=1, source_target_pairs={{0,1},{1,2},{2,3},{4,5},{5,6},{6,7},{8,9},{9,10},{10,11},{12,13},{... | collective-permute-start | bytes 294920 | tf_op jit(solution)/shard_map/ppermute | solution.py:354
  103.6 3.2 %collective-permute-start.5 = (f32[6,32,128]{2,1,0:T(8,128)S(1)}, f32[6,32,128]{2,1,0:T(8,128)S(1)}, u32[]{:S(2)}, u32[]{:S(2)}) collective-permute-start(f32[6,32,128]{2,1,0:T(8,128)S(1)} %get-tuple-element.45), channel_id=1, source_target_pairs={{1,0},{2,1},{3,2},{5,4},{6,5},{7,6},{9,8},{10,9},{11,10},{13,12},{... | collective-permute-start | bytes 294920 | tf_op jit(solution)/shard_map/ppermute | solution.py:354
  107.0 8.0 %collective-permute-start.6 = (f32[6,32,128]{2,1,0:T(8,128)S(1)}, f32[6,32,128]{2,1,0:T(8,128)S(1)}, u32[]{:S(2)}, u32[]{:S(2)}) collective-permute-start(f32[6,32,128]{2,1,0:T(8,128)S(1)} %get-tuple-element.47), channel_id=1, source_target_pairs={{0,4},{1,5},{2,6},{3,7},{4,8},{5,9},{6,10},{7,11},{8,12},{9,13},{1... | collective-permute-start | bytes 294920 | tf_op jit(solution)/shard_map/ppermute | solution.py:349
  110.0 12.2 %collective-permute-start.7 = (f32[6,32,128]{2,1,0:T(8,128)S(1)}, f32[6,32,128]{2,1,0:T(8,128)S(1)}, u32[]{:S(2)}, u32[]{:S(2)}) collective-permute-start(f32[6,32,128]{2,1,0:T(8,128)S(1)} %get-tuple-element.48), channel_id=1, source_target_pairs={{0,28},{1,29},{2,30},{3,31},{4,0},{5,1},{6,2},{7,3},{8,4},{9,5},{1... | collective-permute-start | bytes 294920 | tf_op jit(solution)/shard_map/ppermute | solution.py:349
where the time goes:
time: 147 us; the launch traced here: 146 us
  blocking collectives  79.3 us (54%)
  waiting for transfers between devices  20.9 us (14%)
  starting transfers between devices  20.8 us (14%)
  Pallas kernels  16 us (11%)
  local copies, waits for them, and re-layouts  8.88 us (6%)
    all_to_all x4, blocking collectives, exchange(): return lax.all_to_all(blocks, 'mem', 0, 0, tiled=True).reshape(x.shape)  79.3 us
    ppermute x4, waiting for transfers between devices, along_x(): lax.ppermute(x, 'tile', [(i, (i + by * GRID_Y) % size) for i in range(siz...  15.7 us
    ppermute x4, starting transfers between devices, along_x(): lax.ppermute(x, 'tile', [(i, (i + by * GRID_Y) % size) for i in range(siz...  15.6 us
    unnamed x21, local copies, waits for them, and re-layouts  8.88 us
    pallas_call x2, Pallas kernels, project(): pl.pallas_call(functools.partial(project_kernel, chunks=chunks), in_specs...  6.52 us
    pallas_call x2, Pallas kernels, increment(): pl.pallas_call(functools.partial(increment_kernel, chunks=chunks), in_spe...  6.03 us
    ppermute x4, waiting for transfers between devices, along_y(): lax.ppermute(x, 'tile', [(i, i + by) for i in range(size) if 0 <= i % GRI...  5.2 us
    ppermute x4, starting transfers between devices, along_y(): lax.ppermute(x, 'tile', [(i, i + by) for i in range(size) if 0 <= i % GRI...  5.17 us
  transfers between devices with their start and end apart: 8, of which 6 were waited for; matrix products, arithmetic and copies ran while one was open for 0% of the time, Pallas kernels for 0%

commit v1 on v0

--- a/solution.py
+++ b/solution.py
@@ -8,6 +8,7 @@
 from jax.experimental import pallas as pl
 from jax.experimental.pallas import tpu as pltpu
 from jax.sharding import PartitionSpec as P
+
 
 VARS = 3
 TILE_X = 32
@@ -56,10 +57,57 @@
     return high, (x - high.astype(F32)).astype(BF16)
 
 
-def split_levels_kernel(p_ref, _, o_ref, s_ref, *, own):
-    members, _, levels, _ = p_ref.shape
-    owners = levels // own
-    start = pl.program_id(0) * members
+def in_hbm(x):
+    return pltpu.with_memory_space_constraint(x, pltpu.HBM)
+
+
+def whole(x, space=pltpu.VMEM):
+    zeros = (0,) * x.ndim
+    return pl.BlockSpec(x.shape, lambda k: zeros, memory_space=space)
+
+
+def picked(rows, cols, wanted):
+    row = lax.broadcasted_iota(jnp.int32, (rows, cols), 0)
+    col = lax.broadcasted_iota(jnp.int32, (rows, cols), 1)
+    return jnp.where(row == wanted(col), 1.0, 0.0).astype(F32)
+
+
+def opening_kernel(
+    p_ref, inn_ref, sv_ref, mask_ref, w_ref, kx_ref, ky_ref, mw_ref, m_ref,
+    split_ref, matrix_ref, innov_ref, static_ref, weight_ref, grad_ref, send_ref, cx_ref, cy_ref, scale_ref,
+    s_ref, *, size,
+):
+    own = inn_ref.shape[1]
+    shift = size.bit_length() - 1
+    block, _, levels, _ = p_ref.shape
+    members = mw_ref.shape[1]
+    start = pl.program_id(0) * block
+
+    @pl.when(pl.program_id(0) == 0)
+    def _():
+        for q in range(own):
+            for v in range(VARS):
+                for c in range(CB):
+                    row = (q * VARS + v) * CB + c
+                    lanes = slice(c * LANES, (c + 1) * LANES)
+                    innov_ref[row : row + 1, :] = inn_ref[v, q : q + 1, lanes]
+                    static_ref[row : row + 1, :] = sv_ref[v, q : q + 1, lanes]
+                rows = slice((q * VARS + v) * CB, (q * VARS + v + 1) * CB)
+                weight_ref[rows, :] = mask_ref[...].astype(F32) * w_ref[q, v]
+        grad = weight_ref[...] * (0.0 - innov_ref[...])
+        grad_ref[...] = grad
+        rows = grad.shape[0]
+        for d in range(size):
+            send_ref[d * rows : (d + 1) * rows, :] = grad
+        exact = lax.Precision.HIGHEST
+        lane_bits = LANES.bit_length() - 1
+        level = picked(levels, own * LANES, lambda c: own * (c & (size - 1)) + (c >> lane_bits))
+        member = picked(members, members * size, lambda c: c >> shift)
+        cx_ref[...] = jnp.dot(kx_ref[...], level, precision=exact, preferred_element_type=F32)
+        cy_ref[...] = jnp.dot(ky_ref[...], level, precision=exact, preferred_element_type=F32)
+        scale = jnp.dot(mw_ref[...], member, precision=exact, preferred_element_type=F32)
+        scale_ref[...] = scale / float(size * members)
+        matrix_ref[...] = m_ref[...]
 
     def one(k, carry):
         for v in range(VARS):
@@ -68,32 +116,46 @@
         for v in range(VARS):
             for c in range(CB):
                 for q in range(own):
-                    o_ref[start + k, v, q, c] = s_ref[v * CB + c, pl.ds(q, owners, stride=own), :]
+                    split_ref[start + k, v, q, c] = s_ref[v * CB + c, pl.ds(q, size, stride=own), :]
         return carry
 
-    lax.fori_loop(0, members, one, 0)
-
-
-def split_levels(perturbations, after, own):
+    lax.fori_loop(0, block, one, 0)
+
+
+def opening(perturbations, innovation, static_var, obs_mask, obs_weight, kernel_x, kernel_y, member_weight, size):
     members, _, levels, _ = perturbations.shape
-    step = math.gcd(members, 4)
+    own = levels // size
+    block = math.gcd(members, 4)
+    rows = own * ROWS
+    small = [
+        innovation, static_var, obs_mask.reshape(CB, LANES), obs_weight.T,
+        kernel_x.T, kernel_y.T, member_weight.reshape(1, -1), jnp.asarray(interp_matrix(), BF16),
+    ]
+    specs = [whole(x, pltpu.SMEM if n == 3 else pltpu.VMEM) for n, x in enumerate(small)]
+    shapes = (
+        [jax.ShapeDtypeStruct((members, VARS, own, CB, size, LANES), F32), jax.ShapeDtypeStruct((CELLS, COLS), BF16)]
+        + [jax.ShapeDtypeStruct((rows, LANES), F32)] * 4
+        + [jax.ShapeDtypeStruct((size * rows, LANES), F32)]
+        + [jax.ShapeDtypeStruct((5, own * LANES), F32)] * 2
+        + [jax.ShapeDtypeStruct((1, members * size), F32)]
+    )
     return pl.pallas_call(
-        functools.partial(split_levels_kernel, own=own),
-        grid=(members // step,),
-        in_specs=[
-            pl.BlockSpec((step, VARS, levels, COLS), lambda k: (k, 0, 0, 0)),
-            pl.BlockSpec(memory_space=pl.ANY),
-        ],
-        out_specs=vmem(),
-        out_shape=jax.ShapeDtypeStruct((members, VARS, own, CB, levels // own, LANES), F32),
+        functools.partial(opening_kernel, size=size),
+        grid=(members // block,),
+        in_specs=[pl.BlockSpec((block, VARS, levels, COLS), lambda k: (k, 0, 0, 0))] + specs,
+        out_specs=[vmem()] * len(shapes),
+        out_shape=shapes,
         scratch_shapes=[pltpu.VMEM((VARS * CB, levels, LANES), F32)],
         compiler_params=grant(6),
-        cost_estimate=pl.CostEstimate(flops=400_000_000, bytes_accessed=10_000_000, transcendentals=0),
-        name="split_levels",
-    )(perturbations, after)
-
-
-def project_kernel(p_ref, g_ref, m_ref, c_ref, ylo_ref, yhi_ref, hi_ref, lo_ref, *, chunks):
+        name="opening",
+    )(*[in_hbm(x) for x in [perturbations] + small])
+
+
+def project_kernel(p_ref, g_ref, m_ref, c_ref, near_ref, far_ref, hi_ref, lo_ref, *, chunks):
+    odd = lax.axis_index("tile") % GRID_Y % 2
+    edge = CELLS - 2 * CX
+    near_at = pl.ds(pl.multiple_of((1 - odd) * edge, 8), 2 * CX)
+    far_at = pl.ds(pl.multiple_of(odd * edge, 8), 2 * CX)
     members, _, _, _, owners, _ = p_ref.shape
     tiles = members * owners // LANES
     for n, q in enumerate(chunks):
@@ -121,8 +183,9 @@
         for t in range(tiles):
             piece = coarse[:, t * LANES : (t + 1) * LANES]
             c_ref[n * tiles + t] = piece
-            ylo_ref[n * tiles + t] = piece[: 2 * CX]
-            yhi_ref[n * tiles + t] = piece[CELLS - 2 * CX :]
+        for t in range(n * tiles, (n + 1) * tiles):
+            near_ref[t] = c_ref[t, near_at, :]
+            far_ref[t] = c_ref[t, far_at, :]
 
 
 def project(split, gathered, matrix, chunks):
@@ -146,17 +209,24 @@
     )(split, gathered, matrix)
 
 
-def smooth_y_kernel(c_ref, prev_ref, next_ref, k_ref, s_ref, xlo_ref, xhi_ref, *, chunks):
+def sides(near, far, odd):
+    return jnp.where(odd, near, far), jnp.where(odd, far, near)
+
+
+def smooth_y_kernel(c_ref, near_ref, far_ref, k_ref, s_ref, xnear_ref, xfar_ref, *, chunks):
+    tile = lax.axis_index("tile")
+    odd_y, odd_x = tile % GRID_Y % 2 == 1, tile // GRID_Y % 2 == 1
     tiles = c_ref.shape[0]
     for t in range(tiles):
         q = chunks[t * len(chunks) // tiles]
         coef = [k_ref[d : d + 1, q * LANES : (q + 1) * LANES] for d in range(5)]
+        before, after = sides(near_ref[t], far_ref[t], odd_y)
 
         def rows(b):
             if b < 0:
-                return prev_ref[t, (b + 2) * CX : (b + 3) * CX, :]
+                return before[(b + 2) * CX : (b + 3) * CX, :]
             if b >= CY:
-                return next_ref[t, (b - CY) * CX : (b - CY + 1) * CX, :]
+                return after[(b - CY) * CX : (b - CY + 1) * CX, :]
             return c_ref[t, b * CX : (b + 1) * CX, :]
 
         for b in range(CY):
@@ -165,11 +235,12 @@
                 acc = acc + coef[d] * rows(b + d - 2)
             s_ref[t, b * CX : (b + 1) * CX, :] = acc
         for j in range(2):
-            xlo_ref[t, j * CY : (j + 1) * CY, :] = s_ref[t, pl.ds(j, CY, stride=CX), :]
-            xhi_ref[t, j * CY : (j + 1) * CY, :] = s_ref[t, pl.ds(CX - 2 + j, CY, stride=CX), :]
-
-
-def smooth_y(coarse, from_prev, from_next, coefs, chunks):
+            low = s_ref[t, pl.ds(j, CY, stride=CX), :]
+            high = s_ref[t, pl.ds(CX - 2 + j, CY, stride=CX), :]
+            xnear_ref[t, j * CY : (j + 1) * CY, :], xfar_ref[t, j * CY : (j + 1) * CY, :] = sides(low, high, odd_x)
+
+
+def smooth_y(coarse, near, far, coefs, chunks):
     tiles = coarse.shape[0]
     return pl.pallas_call(
         functools.partial(smooth_y_kernel, chunks=chunks),
@@ -182,10 +253,11 @@
         ],
         compiler_params=grant(2),
         name="smooth_y",
-    )(coarse, from_prev, from_next, coefs)
-
-
-def increment_kernel(p_ref, s_ref, prev_ref, next_ref, k_ref, w_ref, m_ref, o_ref, e_ref, hi_ref, lo_ref, f_ref, *, chunks):
+    )(coarse, near, far, coefs)
+
+
+def increment_kernel(p_ref, s_ref, near_ref, far_ref, k_ref, w_ref, m_ref, o_ref, e_ref, hi_ref, lo_ref, f_ref, *, chunks):
+    odd_x = lax.axis_index("tile") // GRID_Y % 2 == 1
     members, _, _, _, owners, _ = p_ref.shape
     tiles = members * owners // LANES
     for n, q in enumerate(chunks):
@@ -193,9 +265,10 @@
             at = n * tiles + t
             for b in range(CY):
                 e_ref[b * EXT + 8 : b * EXT + 8 + CX, :] = s_ref[at, b * CX : (b + 1) * CX, :]
+            before, after = sides(near_ref[at], far_ref[at], odd_x)
             for j in range(2):
-                e_ref[pl.ds(6 + j, CY, stride=EXT), :] = prev_ref[at, j * CY : (j + 1) * CY, :]
-                e_ref[pl.ds(8 + CX + j, CY, stride=EXT), :] = next_ref[at, j * CY : (j + 1) * CY, :]
+                e_ref[pl.ds(6 + j, CY, stride=EXT), :] = before[j * CY : (j + 1) * CY, :]
+                e_ref[pl.ds(8 + CX + j, CY, stride=EXT), :] = after[j * CY : (j + 1) * CY, :]
             scale = w_ref[:, t * LANES : (t + 1) * LANES]
             coef = [k_ref[d : d + 1, q * LANES : (q + 1) * LANES] * scale for d in range(5)]
             for b in range(CY):
@@ -222,7 +295,7 @@
                 o_ref[pl.ds((n * VARS + v) * CB + c, owners, stride=len(chunks) * ROWS), :] = acc[v]
 
 
-def increment(split, smoothed, from_prev, from_next, coefs, scale, matrix, chunks):
+def increment(split, smoothed, near, far, coefs, scale, matrix, chunks):
     members, _, _, _, owners, _ = split.shape
     return pl.pallas_call(
         functools.partial(increment_kernel, chunks=chunks),
@@ -237,60 +310,7 @@
         ],
         compiler_params=grant(8),
         name="increment",
-    )(split, smoothed, from_prev, from_next, coefs, scale, matrix)
-
-
-def prepare_kernel(
-    inn_ref, sv_ref, mask_ref, w_ref, kx_ref, ky_ref, mw_ref, level_ref, member_ref,
-    innov_ref, static_ref, weight_ref, grad_ref, send_ref, cx_ref, cy_ref, scale_ref,
-    *, norm,
-):
-    own = inn_ref.shape[1]
-    for q in range(own):
-        for v in range(VARS):
-            for c in range(CB):
-                row = (q * VARS + v) * CB + c
-                lanes = slice(c * LANES, (c + 1) * LANES)
-                innov_ref[row : row + 1, :] = inn_ref[v, q : q + 1, lanes]
-                static_ref[row : row + 1, :] = sv_ref[v, q : q + 1, lanes]
-            rows = slice((q * VARS + v) * CB, (q * VARS + v + 1) * CB)
-            weight_ref[rows, :] = mask_ref[...].astype(F32) * w_ref[v, q]
-    grad = weight_ref[...] * (0.0 - innov_ref[...])
-    grad_ref[...] = grad
-    rows = grad.shape[0]
-    for d in range(send_ref.shape[0] // rows):
-        send_ref[d * rows : (d + 1) * rows, :] = grad
-    exact = lax.Precision.HIGHEST
-    cx_ref[...] = jnp.dot(kx_ref[...], level_ref[...], precision=exact, preferred_element_type=F32)
-    cy_ref[...] = jnp.dot(ky_ref[...], level_ref[...], precision=exact, preferred_element_type=F32)
-    scale = jnp.dot(mw_ref[...], member_ref[...], precision=exact, preferred_element_type=F32)
-    scale_ref[...] = scale / norm
-
-
-def prepare(innovation, static_var, obs_mask, obs_weight, kernel_x, kernel_y, member_weight, size):
-    _, own, _ = innovation.shape
-    members, levels = member_weight.shape[0], kernel_x.shape[0]
-    rows = own * ROWS
-    lane = np.arange(own * LANES)
-    level = own * (lane % LANES % size) + lane // LANES
-    pick_level = (np.arange(levels)[:, None] == level[None, :]).astype(np.float32)
-    pick_member = (np.arange(members)[:, None] == np.arange(members * size)[None, :] // size).astype(np.float32)
-    flat = [jax.ShapeDtypeStruct((rows, LANES), F32)] * 4
-    coefs = [jax.ShapeDtypeStruct((5, own * LANES), F32)] * 2
-    return pl.pallas_call(
-        functools.partial(prepare_kernel, norm=float(size * members)),
-        in_specs=[vmem()] * 3 + [pl.BlockSpec(memory_space=pltpu.SMEM)] + [vmem()] * 5,
-        out_specs=[vmem()] * 8,
-        out_shape=flat
-        + [jax.ShapeDtypeStruct((size * rows, LANES), F32)]
-        + coefs
-        + [jax.ShapeDtypeStruct((1, members * size), F32)],
-        compiler_params=grant(2),
-        name="prepare",
-    )(
-        innovation, static_var, obs_mask.reshape(CB, LANES), obs_weight, kernel_x.T, kernel_y.T,
-        member_weight.reshape(1, -1), jnp.asarray(pick_level), jnp.asarray(pick_member),
-    )
+    )(split, smoothed, near, far, coefs, scale, matrix)
 
 
 def update_kernel(r_ref, *refs, size, last):
@@ -344,34 +364,36 @@
     return lax.all_to_all(blocks, "mem", 0, 0, tiled=True).reshape(x.shape)
 
 
-def along_x(x, by):
-    size = lax.axis_size("tile")
-    return lax.ppermute(x, "tile", [(i, (i + by * GRID_Y) % size) for i in range(size)])
-
-
-def along_y(x, by):
-    size = lax.axis_size("tile")
-    return lax.ppermute(x, "tile", [(i, i + by) for i in range(size) if 0 <= i % GRID_Y + by < GRID_Y])
+def swapped(near, far, stride, places, periodic):
+    def pairs(is_near):
+        out = []
+        for i in range(lax.axis_size("tile")):
+            place = i // stride % places
+            to = place + (1 if (place % 2 == 0) == is_near else -1)
+            if periodic or 0 <= to < places:
+                out.append((i, i + (to % places - place) * stride))
+        return out
+
+    from_far = lax.ppermute(far, "tile", pairs(False))
+    from_near = lax.ppermute(near, "tile", pairs(True))
+    return from_near, from_far
 
 
 def body(perturbations, member_weight, innovation, obs_weight, static_var, obs_mask, kernel_x, kernel_y):
     size = lax.axis_size("mem")
-    own = perturbations.shape[2] // size
-    chunks = tuple(range(own))
-    matrix = jnp.asarray(interp_matrix(), BF16)
-    innov, static, weight, gradient, to_send, coef_x, coef_y, scale = prepare(
-        innovation, static_var, obs_mask, obs_weight, kernel_x, kernel_y, member_weight, size
+    grid_x = lax.axis_size("tile") // GRID_Y
+    chunks = tuple(range(perturbations.shape[2] // size))
+    split, matrix, innov, static, weight, gradient, to_send, coef_x, coef_y, scale = opening(
+        perturbations, innovation, static_var, obs_mask, obs_weight, kernel_x, kernel_y, member_weight, size
     )
-    analysis = split = None
+    analysis = None
     for step in range(STEPS):
         gathered = exchange(to_send, size)
-        if split is None:
-            split = split_levels(perturbations, gathered, own)
-        coarse, ylo, yhi = project(split, gathered, matrix, chunks)
-        from_prev, from_next = along_y(yhi, 1), along_y(ylo, -1)
-        smoothed, xlo, xhi = smooth_y(coarse, from_prev, from_next, coef_y, chunks)
-        from_prev, from_next = along_x(xhi, 1), along_x(xlo, -1)
-        partial = increment(split, smoothed, from_prev, from_next, coef_x, scale, matrix, chunks)
+        coarse, near, far = project(split, gathered, matrix, chunks)
+        near, far = swapped(near, far, 1, GRID_Y, False)
+        smoothed, near, far = smooth_y(coarse, near, far, coef_y, chunks)
+        near, far = swapped(near, far, GRID_Y, grid_x, True)
+        partial = increment(split, smoothed, near, far, coef_x, scale, matrix, chunks)
         received = exchange(partial, size)
         if step == STEPS - 1:
             return update(received, (analysis, gradient, static), size, True)[0]

time: 147 us -> 138 us (0.939)
  the two profiles are of different devices: /device:TPU:12 before, /device:TPU:1 now
where the time goes in v1:
time: 138 us; the launch traced here: 137 us
  blocking collectives  67.7 us (49%)
  starting transfers between devices  38 us (28%)
  Pallas kernels  19.1 us (14%)
  waiting for transfers between devices  12 us (9%)
    all_to_all x4, blocking collectives, exchange(): return lax.all_to_all(blocks, 'mem', 0, 0, tiled=True).reshape(x.shape)  67.7 us
    ppermute x4, starting transfers between devices, swapped(): from_far = lax.ppermute(far, 'tile', pairs(False))  24.6 us
    ppermute x4, starting transfers between devices, swapped(): from_near = lax.ppermute(near, 'tile', pairs(True))  13.4 us
    ppermute x4, waiting for transfers between devices, swapped(): from_far = lax.ppermute(far, 'tile', pairs(False))  12 us
    pallas_call x2, Pallas kernels, project(): pl.pallas_call(functools.partial(project_kernel, chunks=chunks), in_specs...  6.66 us
    pallas_call x2, Pallas kernels, increment(): pl.pallas_call(functools.partial(increment_kernel, chunks=chunks), in_spe...  6.09 us
    pallas_call x1, Pallas kernels, opening(): pl.pallas_call(functools.partial(opening_kernel, size=size), grid=(member...  5.03 us
  transfers between devices with their start and end apart: 8, of which 4 were waited for; matrix products, arithmetic and copies ran while one was open for 0% of the time, Pallas kernels for 0%

profile of v1, /device:TPU:1, one launch (start us, length us, event | category | flops | bytes accessed | tf_op | source)
XLA Modules:
  0.0 137.0 jit_solution(18018488133571694033)
XLA Ops:
  0.0 5.0 %opening.1 = (f32[24,3,2,8,16,128]{5,4,3,2,1,0:T(8,128)S(1)}, bf16[256,1024]{1,0:T(8,128)(2,1)S(1)}, f32[48,128]{1,0:T(8,128)S(1)}, f32[48,128]{1,0:T(8,128)S(1)...) custom-call(bf16[24,3,32,1024]{3,2,1,0:T(8,128)(2,1)} %p_ref.1, ...), custom_call_target="tpu_custom_call" | custom-call | tf_op jit(solution)/shard_map/opening/pallas_call | solution.py:142
  5.0 20.4 %all_to_all.20 = f32[16,48,128]{2,1,0:T(8,128)S(1)} all-to-all(f32[16,48,128]{2,1,0:T(8,128)S(1)} %bitcast.19), channel_id=1, replica_groups=mesh['mem'=16,'tile'=32] {'mem'}, dimensions={0} | all-to-all | bytes 786432 | tf_op jit(solution)/shard_map/all_to_all | solution.py:364
  25.4 3.3 %project.2 = (f32[6,256,128]{2,1,0:T(8,128)S(1)}, f32[6,32,128]{2,1,0:T(8,128)S(1)}, f32[6,32,128]{2,1,0:T(8,128)S(1)}) custom-call(f32[24,3,2,8,16,128]{5,4,3,2,1,0:T(8,128)S(1)} %get-tuple-element.30.p_ref, f32[768,128]{1,0:T(8,128)S(1)} %bitcast.13, bf16[256,1024]{1,0:T(8,128)(2,1)S(1)} %get-tuple-element.32.m_ref), custom_call_target="tpu_custom_call" | custom-call | tf_op jit(solution)/shard_map/project/pallas_call | solution.py:194
  28.7 4.5 %collective-permute-start = (f32[6,32,128]{2,1,0:T(8,128)S(1)}, f32[6,32,128]{2,1,0:T(8,128)S(1)}, u32[]{:S(2)}, u32[]{:S(2)}) collective-permute-start(f32[6,32,128]{2,1,0:T(8,128)S(1)} %get-tuple-element.34), channel_id=1, source_target_pairs={{0,1},{1,0},{2,3},{3,2},{4,5},{5,4},{6,7},{7,6},{8,9},{9,8},{10,11... | collective-permute-start | bytes 294920 | tf_op jit(solution)/shard_map/ppermute | solution.py:378
  33.2 3.0 %collective-permute-start.1 = (f32[6,32,128]{2,1,0:T(8,128)S(1)}, f32[6,32,128]{2,1,0:T(8,128)S(1)}, u32[]{:S(2)}, u32[]{:S(2)}) collective-permute-start(f32[6,32,128]{2,1,0:T(8,128)S(1)} %get-tuple-element.35), channel_id=1, source_target_pairs={{1,2},{2,1},{5,6},{6,5},{9,10},{10,9},{13,14},{14,13},{17,18},{18,... | collective-permute-start | bytes 294920 | tf_op jit(solution)/shard_map/ppermute | solution.py:377
  36.2 2.9 %collective-permute-done.1.far_ref = f32[6,32,128]{2,1,0:T(8,128)S(1)} collective-permute-done((f32[6,32,128]{2,1,0:T(8,128)S(1)}, f32[6,32,128]{2,1,0:T(8,128)S(1)}, u32[]{:S(2)}, u32[]{:S(2)}) %collective-permute-start.1) | collective-permute-done | bytes 98336 | tf_op jit(solution)/shard_map/ppermute | solution.py:377
  39.1 0.3 smooth_y.2
  39.5 4.6 %collective-permute-start.2 = (f32[6,32,128]{2,1,0:T(8,128)S(1)}, f32[6,32,128]{2,1,0:T(8,128)S(1)}, u32[]{:S(2)}, u32[]{:S(2)}) collective-permute-start(f32[6,32,128]{2,1,0:T(8,128)S(1)} %get-tuple-element.38), channel_id=1, source_target_pairs={{0,4},{1,5},{2,6},{3,7},{4,0},{5,1},{6,2},{7,3},{8,12},{9,13},{10,... | collective-permute-start | bytes 294920 | tf_op jit(solution)/shard_map/ppermute | solution.py:378
  44.1 9.7 %collective-permute-start.3 = (f32[6,32,128]{2,1,0:T(8,128)S(1)}, f32[6,32,128]{2,1,0:T(8,128)S(1)}, u32[]{:S(2)}, u32[]{:S(2)}) collective-permute-start(f32[6,32,128]{2,1,0:T(8,128)S(1)} %get-tuple-element.39), channel_id=1, source_target_pairs={{0,28},{1,29},{2,30},{3,31},{4,8},{5,9},{6,10},{7,11},{8,4},{9,5},... | collective-permute-start | bytes 294920 | tf_op jit(solution)/shard_map/ppermute | solution.py:377
  53.8 2.6 %collective-permute-done.3.far_ref = f32[6,32,128]{2,1,0:T(8,128)S(1)} collective-permute-done((f32[6,32,128]{2,1,0:T(8,128)S(1)}, f32[6,32,128]{2,1,0:T(8,128)S(1)}, u32[]{:S(2)}, u32[]{:S(2)}) %collective-permute-start.3) | collective-permute-done | bytes 98336 | tf_op jit(solution)/shard_map/ppermute | solution.py:377
  56.4 3.0 %increment.2 = f32[768,128]{1,0:T(8,128)S(1)} custom-call(f32[24,3,2,8,16,128]{5,4,3,2,1,0:T(8,128)S(1)} %get-tuple-element.30.p_ref, f32[6,256,128]{2,1,0:T(8,128)S(1)} %get-tuple-element.37.s_ref, f32[6,32,128]{2,1,0:T(8,128)S(1)} %collective-permute-done.2.near_ref, f32[6,32,128]{2,1,0:T(8,128)S(1)} %collective-permute-done.3.far_ref, ...), custom_call_target="tpu_custom_call" | custom-call | tf_op jit(solution)/shard_map/increment/pallas_call | solution.py:300
  59.5 14.8 %all_to_all.21 = f32[16,48,128]{2,1,0:T(8,128)S(1)} all-to-all(f32[16,48,128]{2,1,0:T(8,128)S(1)} %bitcast.18), channel_id=1, replica_groups=mesh['mem'=16,'tile'=32] {'mem'}, dimensions={0} | all-to-all | bytes 786432 | tf_op jit(solution)/shard_map/all_to_all | solution.py:364
  74.3 18.1 %all_to_all.22 = f32[16,48,128]{2,1,0:T(8,128)S(1)} all-to-all(f32[16,48,128]{2,1,0:T(8,128)S(1)} %bitcast.20), channel_id=1, replica_groups=mesh['mem'=16,'tile'=32] {'mem'}, dimensions={0} | all-to-all | bytes 786432 | tf_op jit(solution)/shard_map/all_to_all | solution.py:364
  92.4 3.3 %project.3 = (f32[6,256,128]{2,1,0:T(8,128)S(1)}, f32[6,32,128]{2,1,0:T(8,128)S(1)}, f32[6,32,128]{2,1,0:T(8,128)S(1)}) custom-call(f32[24,3,2,8,16,128]{5,4,3,2,1,0:T(8,128)S(1)} %get-tuple-element.30.p_ref, f32[768,128]{1,0:T(8,128)S(1)} %bitcast.14, bf16[256,1024]{1,0:T(8,128)(2,1)S(1)} %get-tuple-element.32.m_ref), custom_call_target="tpu_custom_call" | custom-call | tf_op jit(solution)/shard_map/project/pallas_call | solution.py:194
  95.7 2.4 %collective-permute-start.4 = (f32[6,32,128]{2,1,0:T(8,128)S(1)}, f32[6,32,128]{2,1,0:T(8,128)S(1)}, u32[]{:S(2)}, u32[]{:S(2)}) collective-permute-start(f32[6,32,128]{2,1,0:T(8,128)S(1)} %get-tuple-element.48), channel_id=1, source_target_pairs={{0,1},{1,0},{2,3},{3,2},{4,5},{5,4},{6,7},{7,6},{8,9},{9,8},{10,11... | collective-permute-start | bytes 294920 | tf_op jit(solution)/shard_map/ppermute | solution.py:378
  98.1 1.9 %collective-permute-start.5 = (f32[6,32,128]{2,1,0:T(8,128)S(1)}, f32[6,32,128]{2,1,0:T(8,128)S(1)}, u32[]{:S(2)}, u32[]{:S(2)}) collective-permute-start(f32[6,32,128]{2,1,0:T(8,128)S(1)} %get-tuple-element.49), channel_id=1, source_target_pairs={{1,2},{2,1},{5,6},{6,5},{9,10},{10,9},{13,14},{14,13},{17,18},{18,... | collective-permute-start | bytes 294920 | tf_op jit(solution)/shard_map/ppermute | solution.py:377
  100.0 4.0 %collective-permute-done.5.far_ref = f32[6,32,128]{2,1,0:T(8,128)S(1)} collective-permute-done((f32[6,32,128]{2,1,0:T(8,128)S(1)}, f32[6,32,128]{2,1,0:T(8,128)S(1)}, u32[]{:S(2)}, u32[]{:S(2)}) %collective-permute-start.5) | collective-permute-done | bytes 98336 | tf_op jit(solution)/shard_map/ppermute | solution.py:377
  104.0 0.3 smooth_y.3
  104.4 1.9 %collective-permute-start.6 = (f32[6,32,128]{2,1,0:T(8,128)S(1)}, f32[6,32,128]{2,1,0:T(8,128)S(1)}, u32[]{:S(2)}, u32[]{:S(2)}) collective-permute-start(f32[6,32,128]{2,1,0:T(8,128)S(1)} %get-tuple-element.51), channel_id=1, source_target_pairs={{0,4},{1,5},{2,6},{3,7},{4,0},{5,1},{6,2},{7,3},{8,12},{9,13},{10,... | collective-permute-start | bytes 294920 | tf_op jit(solution)/shard_map/ppermute | solution.py:378
  106.3 10.0 %collective-permute-start.7 = (f32[6,32,128]{2,1,0:T(8,128)S(1)}, f32[6,32,128]{2,1,0:T(8,128)S(1)}, u32[]{:S(2)}, u32[]{:S(2)}) collective-permute-start(f32[6,32,128]{2,1,0:T(8,128)S(1)} %get-tuple-element.52), channel_id=1, source_target_pairs={{0,28},{1,29},{2,30},{3,31},{4,8},{5,9},{6,10},{7,11},{8,4},{9,5},... | collective-permute-start | bytes 294920 | tf_op jit(solution)/shard_map/ppermute | solution.py:377
  116.3 2.6 %collective-permute-done.7.far_ref = f32[6,32,128]{2,1,0:T(8,128)S(1)} collective-permute-done((f32[6,32,128]{2,1,0:T(8,128)S(1)}, f32[6,32,128]{2,1,0:T(8,128)S(1)}, u32[]{:S(2)}, u32[]{:S(2)}) %collective-permute-start.7) | collective-permute-done | bytes 98336 | tf_op jit(solution)/shard_map/ppermute | solution.py:377
  118.8 3.0 %increment.3 = f32[768,128]{1,0:T(8,128)S(1)} custom-call(f32[24,3,2,8,16,128]{5,4,3,2,1,0:T(8,128)S(1)} %get-tuple-element.30.p_ref, f32[6,256,128]{2,1,0:T(8,128)S(1)} %get-tuple-element.50.s_ref, f32[6,32,128]{2,1,0:T(8,128)S(1)} %collective-permute-done.6.near_ref, f32[6,32,128]{2,1,0:T(8,128)S(1)} %collective-permute-done.7.far_ref, ...), custom_call_target="tpu_custom_call" | custom-call | tf_op jit(solution)/shard_map/increment/pallas_call | solution.py:300
  121.9 14.5 %all_to_all.23 = f32[16,48,128]{2,1,0:T(8,128)S(1)} all-to-all(f32[16,48,128]{2,1,0:T(8,128)S(1)} %bitcast.17), channel_id=1, replica_groups=mesh['mem'=16,'tile'=32] {'mem'}, dimensions={0} | all-to-all | bytes 786432 | tf_op jit(solution)/shard_map/all_to_all | solution.py:364
  136.3 0.7 update.3
  (5 shorter events, 0.1 us)
Async XLA Ops:
  28.7 7.5 %collective-permute-start = (f32[6,32,128]{2,1,0:T(8,128)S(1)}, f32[6,32,128]{2,1,0:T(8,128)S(1)}, u32[]{:S(2)}, u32[]{:S(2)}) collective-permute-start(f32[6,32,128]{2,1,0:T(8,128)S(1)} %get-tuple-element.34), channel_id=1, source_target_pairs={{0,1},{1,0},{2,3},{3,2},{4,5},{5,4},{6,7},{7,6},{8,9},{9,8},{10,11... | collective-permute-start | bytes 294920 | tf_op jit(solution)/shard_map/ppermute | solution.py:378
  33.2 5.9 %collective-permute-start.1 = (f32[6,32,128]{2,1,0:T(8,128)S(1)}, f32[6,32,128]{2,1,0:T(8,128)S(1)}, u32[]{:S(2)}, u32[]{:S(2)}) collective-permute-start(f32[6,32,128]{2,1,0:T(8,128)S(1)} %get-tuple-element.35), channel_id=1, source_target_pairs={{1,2},{2,1},{5,6},{6,5},{9,10},{10,9},{13,14},{14,13},{17,18},{18,... | collective-permute-start | bytes 294920 | tf_op jit(solution)/shard_map/ppermute | solution.py:377
  39.5 14.4 %collective-permute-start.2 = (f32[6,32,128]{2,1,0:T(8,128)S(1)}, f32[6,32,128]{2,1,0:T(8,128)S(1)}, u32[]{:S(2)}, u32[]{:S(2)}) collective-permute-start(f32[6,32,128]{2,1,0:T(8,128)S(1)} %get-tuple-element.38), channel_id=1, source_target_pairs={{0,4},{1,5},{2,6},{3,7},{4,0},{5,1},{6,2},{7,3},{8,12},{9,13},{10,... | collective-permute-start | bytes 294920 | tf_op jit(solution)/shard_map/ppermute | solution.py:378
  44.1 12.3 %collective-permute-start.3 = (f32[6,32,128]{2,1,0:T(8,128)S(1)}, f32[6,32,128]{2,1,0:T(8,128)S(1)}, u32[]{:S(2)}, u32[]{:S(2)}) collective-permute-start(f32[6,32,128]{2,1,0:T(8,128)S(1)} %get-tuple-element.39), channel_id=1, source_target_pairs={{0,28},{1,29},{2,30},{3,31},{4,8},{5,9},{6,10},{7,11},{8,4},{9,5},... | collective-permute-start | bytes 294920 | tf_op jit(solution)/shard_map/ppermute | solution.py:377
  95.7 4.3 %collective-permute-start.4 = (f32[6,32,128]{2,1,0:T(8,128)S(1)}, f32[6,32,128]{2,1,0:T(8,128)S(1)}, u32[]{:S(2)}, u32[]{:S(2)}) collective-permute-start(f32[6,32,128]{2,1,0:T(8,128)S(1)} %get-tuple-element.48), channel_id=1, source_target_pairs={{0,1},{1,0},{2,3},{3,2},{4,5},{5,4},{6,7},{7,6},{8,9},{9,8},{10,11... | collective-permute-start | bytes 294920 | tf_op jit(solution)/shard_map/ppermute | solution.py:378
  98.1 5.9 %collective-permute-start.5 = (f32[6,32,128]{2,1,0:T(8,128)S(1)}, f32[6,32,128]{2,1,0:T(8,128)S(1)}, u32[]{:S(2)}, u32[]{:S(2)}) collective-permute-start(f32[6,32,128]{2,1,0:T(8,128)S(1)} %get-tuple-element.49), channel_id=1, source_target_pairs={{1,2},{2,1},{5,6},{6,5},{9,10},{10,9},{13,14},{14,13},{17,18},{18,... | collective-permute-start | bytes 294920 | tf_op jit(solution)/shard_map/ppermute | solution.py:377
  104.4 11.9 %collective-permute-start.6 = (f32[6,32,128]{2,1,0:T(8,128)S(1)}, f32[6,32,128]{2,1,0:T(8,128)S(1)}, u32[]{:S(2)}, u32[]{:S(2)}) collective-permute-start(f32[6,32,128]{2,1,0:T(8,128)S(1)} %get-tuple-element.51), channel_id=1, source_target_pairs={{0,4},{1,5},{2,6},{3,7},{4,0},{5,1},{6,2},{7,3},{8,12},{9,13},{10,... | collective-permute-start | bytes 294920 | tf_op jit(solution)/shard_map/ppermute | solution.py:378
  106.3 12.5 %collective-permute-start.7 = (f32[6,32,128]{2,1,0:T(8,128)S(1)}, f32[6,32,128]{2,1,0:T(8,128)S(1)}, u32[]{:S(2)}, u32[]{:S(2)}) collective-permute-start(f32[6,32,128]{2,1,0:T(8,128)S(1)} %get-tuple-element.52), channel_id=1, source_target_pairs={{0,28},{1,29},{2,30},{3,31},{4,8},{5,9},{6,10},{7,11},{8,4},{9,5},... | collective-permute-start | bytes 294920 | tf_op jit(solution)/shard_map/ppermute | solution.py:377

commit v2 on v1

--- a/solution.py
+++ b/solution.py
@@ -171,15 +171,15 @@
                 for v in range(1, VARS):
                     acc = acc + p_ref[k, v, q, c] * grad[v]
                 high, low = split_terms(acc)
-                at = pl.ds(pl.multiple_of(k * owners, owners), owners)
-                hi_ref[at, lanes] = high
-                lo_ref[at, lanes] = low
+                at = pl.ds(k * owners, owners)
+                hi_ref[n, at, lanes] = high
+                lo_ref[n, at, lanes] = low
                 return carry
 
-            lax.fori_loop(0, members, one, 0, unroll=4)
+            lax.fori_loop(0, members, one, 0, unroll=True)
         dims = (((1,), (1,)), ((), ()))
-        coarse = lax.dot_general(m_ref[...], hi_ref[...], dims, preferred_element_type=F32)
-        coarse = coarse + lax.dot_general(m_ref[...], lo_ref[...], dims, preferred_element_type=F32)
+        coarse = lax.dot_general(m_ref[...], hi_ref[n], dims, preferred_element_type=F32)
+        coarse = coarse + lax.dot_general(m_ref[...], lo_ref[n], dims, preferred_element_type=F32)
         for t in range(tiles):
             piece = coarse[:, t * LANES : (t + 1) * LANES]
             c_ref[n * tiles + t] = piece
@@ -201,8 +201,8 @@
             jax.ShapeDtypeStruct((tiles, 2 * CX, LANES), F32),
         ],
         scratch_shapes=[
-            pltpu.VMEM((members * owners, COLS), BF16),
-            pltpu.VMEM((members * owners, COLS), BF16),
+            pltpu.VMEM((len(chunks), members * owners, COLS), BF16),
+            pltpu.VMEM((len(chunks), members * owners, COLS), BF16),
         ],
         compiler_params=grant(8),
         name="project",
@@ -264,33 +264,33 @@
         for t in range(tiles):
             at = n * tiles + t
             for b in range(CY):
-                e_ref[b * EXT + 8 : b * EXT + 8 + CX, :] = s_ref[at, b * CX : (b + 1) * CX, :]
+                e_ref[at, b * EXT + 8 : b * EXT + 8 + CX, :] = s_ref[at, b * CX : (b + 1) * CX, :]
             before, after = sides(near_ref[at], far_ref[at], odd_x)
             for j in range(2):
-                e_ref[pl.ds(6 + j, CY, stride=EXT), :] = before[j * CY : (j + 1) * CY, :]
-                e_ref[pl.ds(8 + CX + j, CY, stride=EXT), :] = after[j * CY : (j + 1) * CY, :]
+                e_ref[at, pl.ds(6 + j, CY, stride=EXT), :] = before[j * CY : (j + 1) * CY, :]
+                e_ref[at, pl.ds(8 + CX + j, CY, stride=EXT), :] = after[j * CY : (j + 1) * CY, :]
             scale = w_ref[:, t * LANES : (t + 1) * LANES]
             coef = [k_ref[d : d + 1, q * LANES : (q + 1) * LANES] * scale for d in range(5)]
             for b in range(CY):
-                acc = coef[0] * e_ref[b * EXT + 6 : b * EXT + 6 + CX, :]
+                acc = coef[0] * e_ref[at, b * EXT + 6 : b * EXT + 6 + CX, :]
                 for d in range(1, 5):
-                    acc = acc + coef[d] * e_ref[b * EXT + 6 + d : b * EXT + 6 + d + CX, :]
+                    acc = acc + coef[d] * e_ref[at, b * EXT + 6 + d : b * EXT + 6 + d + CX, :]
                 high, low = split_terms(acc)
-                hi_ref[b * CX : (b + 1) * CX, t * LANES : (t + 1) * LANES] = high
-                lo_ref[b * CX : (b + 1) * CX, t * LANES : (t + 1) * LANES] = low
+                hi_ref[n, b * CX : (b + 1) * CX, t * LANES : (t + 1) * LANES] = high
+                lo_ref[n, b * CX : (b + 1) * CX, t * LANES : (t + 1) * LANES] = low
         dims = (((0,), (0,)), ((), ()))
-        fine = lax.dot_general(hi_ref[...], m_ref[...], dims, preferred_element_type=F32)
-        f_ref[...] = fine + lax.dot_general(lo_ref[...], m_ref[...], dims, preferred_element_type=F32)
+        fine = lax.dot_general(hi_ref[n], m_ref[...], dims, preferred_element_type=F32)
+        f_ref[n] = fine + lax.dot_general(lo_ref[n], m_ref[...], dims, preferred_element_type=F32)
         for c in range(CB):
             lanes = slice(c * LANES, (c + 1) * LANES)
 
             def one(k, acc):
-                at = pl.ds(pl.multiple_of(k * owners, owners), owners)
-                local = f_ref[at, lanes]
+                at = pl.ds(k * owners, owners)
+                local = f_ref[n, at, lanes]
                 return tuple(acc[v] + p_ref[k, v, q, c] * local for v in range(VARS))
 
             zero = jnp.zeros((owners, LANES), F32)
-            acc = lax.fori_loop(0, members, one, (zero,) * VARS, unroll=4)
+            acc = lax.fori_loop(0, members, one, (zero,) * VARS, unroll=True)
             for v in range(VARS):
                 o_ref[pl.ds((n * VARS + v) * CB + c, owners, stride=len(chunks) * ROWS), :] = acc[v]
 
@@ -303,10 +303,10 @@
         out_specs=vmem(),
         out_shape=jax.ShapeDtypeStruct((owners * len(chunks) * ROWS, LANES), F32),
         scratch_shapes=[
-            pltpu.VMEM((CY * EXT + 8, LANES), F32),
-            pltpu.VMEM((CELLS, members * owners), BF16),
-            pltpu.VMEM((CELLS, members * owners), BF16),
-            pltpu.VMEM((members * owners, COLS), F32),
+            pltpu.VMEM((smoothed.shape[0], CY * EXT + 8, LANES), F32),
+            pltpu.VMEM((len(chunks), CELLS, members * owners), BF16),
+            pltpu.VMEM((len(chunks), CELLS, members * owners), BF16),
+            pltpu.VMEM((len(chunks), members * owners, COLS), F32),
         ],
         compiler_params=grant(8),
         name="increment",

time: 138 us -> 133 us (0.964)
  Pallas kernels: 19.1 us -> 14.9 us
    pallas_call x2, Pallas kernels: 6.66 us -> 4.46 us  [project(): pl.pallas_call(functools.partial(project_kernel, chunks=chunks), in_specs...]
    pallas_call x2, Pallas kernels: 6.09 us -> 4.08 us  [increment(): pl.pallas_call(functools.partial(increment_kernel, chunks=chunks), in_spe...]
where the time goes in v2:
time: 133 us
  blocking collectives  67.7 us (51%)
  starting transfers between devices  38 us (29%)
  Pallas kernels  14.9 us (11%)
  waiting for transfers between devices  12 us (9%)
    all_to_all x4, blocking collectives, exchange(): return lax.all_to_all(blocks, 'mem', 0, 0, tiled=True).reshape(x.shape)  67.7 us
    ppermute x4, starting transfers between devices, swapped(): from_far = lax.ppermute(far, 'tile', pairs(False))  24.6 us
    ppermute x4, starting transfers between devices, swapped(): from_near = lax.ppermute(near, 'tile', pairs(True))  13.4 us
    ppermute x4, waiting for transfers between devices, swapped(): from_far = lax.ppermute(far, 'tile', pairs(False))  12 us
    pallas_call x1, Pallas kernels, opening(): pl.pallas_call(functools.partial(opening_kernel, size=size), grid=(member...  5.03 us
    pallas_call x2, Pallas kernels, project(): pl.pallas_call(functools.partial(project_kernel, chunks=chunks), in_specs...  4.46 us
    pallas_call x2, Pallas kernels, increment(): pl.pallas_call(functools.partial(increment_kernel, chunks=chunks), in_spe...  4.08 us
  transfers between devices with their start and end apart: 8, of which 4 were waited for; matrix products, arithmetic and copies ran while one was open for 0% of the time, Pallas kernels for 0%

profile of v2, /device:TPU:1, one launch (start us, length us, event | category | flops | bytes accessed | tf_op | source)
XLA Modules:
  0.0 132.8 jit_solution(6488475018424613196)
XLA Ops:
  0.0 5.0 %opening.1 = (f32[24,3,2,8,16,128]{5,4,3,2,1,0:T(8,128)S(1)}, bf16[256,1024]{1,0:T(8,128)(2,1)S(1)}, f32[48,128]{1,0:T(8,128)S(1)}, f32[48,128]{1,0:T(8,128)S(1)...) custom-call(bf16[24,3,32,1024]{3,2,1,0:T(8,128)(2,1)} %p_ref.1, ...), custom_call_target="tpu_custom_call" | custom-call | tf_op jit(solution)/shard_map/opening/pallas_call | solution.py:142
  5.0 20.4 %all_to_all.20 = f32[16,48,128]{2,1,0:T(8,128)S(1)} all-to-all(f32[16,48,128]{2,1,0:T(8,128)S(1)} %bitcast.19), channel_id=1, replica_groups=mesh['mem'=16,'tile'=32] {'mem'}, dimensions={0} | all-to-all | bytes 786432 | tf_op jit(solution)/shard_map/all_to_all | solution.py:364
  25.4 2.2 %project.2 = (f32[6,256,128]{2,1,0:T(8,128)S(1)}, f32[6,32,128]{2,1,0:T(8,128)S(1)}, f32[6,32,128]{2,1,0:T(8,128)S(1)}) custom-call(f32[24,3,2,8,16,128]{5,4,3,2,1,0:T(8,128)S(1)} %get-tuple-element.30.p_ref, f32[768,128]{1,0:T(8,128)S(1)} %bitcast.13, bf16[256,1024]{1,0:T(8,128)(2,1)S(1)} %get-tuple-element.32.m_ref), custom_call_target="tpu_custom_call" | custom-call | tf_op jit(solution)/shard_map/project/pallas_call | solution.py:194
  27.6 4.5 %collective-permute-start = (f32[6,32,128]{2,1,0:T(8,128)S(1)}, f32[6,32,128]{2,1,0:T(8,128)S(1)}, u32[]{:S(2)}, u32[]{:S(2)}) collective-permute-start(f32[6,32,128]{2,1,0:T(8,128)S(1)} %get-tuple-element.34), channel_id=1, source_target_pairs={{0,1},{1,0},{2,3},{3,2},{4,5},{5,4},{6,7},{7,6},{8,9},{9,8},{10,11... | collective-permute-start | bytes 294920 | tf_op jit(solution)/shard_map/ppermute | solution.py:378
  32.1 3.0 %collective-permute-start.1 = (f32[6,32,128]{2,1,0:T(8,128)S(1)}, f32[6,32,128]{2,1,0:T(8,128)S(1)}, u32[]{:S(2)}, u32[]{:S(2)}) collective-permute-start(f32[6,32,128]{2,1,0:T(8,128)S(1)} %get-tuple-element.35), channel_id=1, source_target_pairs={{1,2},{2,1},{5,6},{6,5},{9,10},{10,9},{13,14},{14,13},{17,18},{18,... | collective-permute-start | bytes 294920 | tf_op jit(solution)/shard_map/ppermute | solution.py:377
  35.1 2.9 %collective-permute-done.1.far_ref = f32[6,32,128]{2,1,0:T(8,128)S(1)} collective-permute-done((f32[6,32,128]{2,1,0:T(8,128)S(1)}, f32[6,32,128]{2,1,0:T(8,128)S(1)}, u32[]{:S(2)}, u32[]{:S(2)}) %collective-permute-start.1) | collective-permute-done | bytes 98336 | tf_op jit(solution)/shard_map/ppermute | solution.py:377
  38.0 0.3 smooth_y.2
  38.4 4.7 %collective-permute-start.2 = (f32[6,32,128]{2,1,0:T(8,128)S(1)}, f32[6,32,128]{2,1,0:T(8,128)S(1)}, u32[]{:S(2)}, u32[]{:S(2)}) collective-permute-start(f32[6,32,128]{2,1,0:T(8,128)S(1)} %get-tuple-element.38), channel_id=1, source_target_pairs={{0,4},{1,5},{2,6},{3,7},{4,0},{5,1},{6,2},{7,3},{8,12},{9,13},{10,... | collective-permute-start | bytes 294920 | tf_op jit(solution)/shard_map/ppermute | solution.py:378
  43.0 9.7 %collective-permute-start.3 = (f32[6,32,128]{2,1,0:T(8,128)S(1)}, f32[6,32,128]{2,1,0:T(8,128)S(1)}, u32[]{:S(2)}, u32[]{:S(2)}) collective-permute-start(f32[6,32,128]{2,1,0:T(8,128)S(1)} %get-tuple-element.39), channel_id=1, source_target_pairs={{0,28},{1,29},{2,30},{3,31},{4,8},{5,9},{6,10},{7,11},{8,4},{9,5},... | collective-permute-start | bytes 294920 | tf_op jit(solution)/shard_map/ppermute | solution.py:377
  52.7 2.6 %collective-permute-done.3.far_ref = f32[6,32,128]{2,1,0:T(8,128)S(1)} collective-permute-done((f32[6,32,128]{2,1,0:T(8,128)S(1)}, f32[6,32,128]{2,1,0:T(8,128)S(1)}, u32[]{:S(2)}, u32[]{:S(2)}) %collective-permute-start.3) | collective-permute-done | bytes 98336 | tf_op jit(solution)/shard_map/ppermute | solution.py:377
  55.3 2.0 %increment.2 = f32[768,128]{1,0:T(8,128)S(1)} custom-call(f32[24,3,2,8,16,128]{5,4,3,2,1,0:T(8,128)S(1)} %get-tuple-element.30.p_ref, f32[6,256,128]{2,1,0:T(8,128)S(1)} %get-tuple-element.37.s_ref, f32[6,32,128]{2,1,0:T(8,128)S(1)} %collective-permute-done.2.near_ref, f32[6,32,128]{2,1,0:T(8,128)S(1)} %collective-permute-done.3.far_ref, ...), custom_call_target="tpu_custom_call" | custom-call | tf_op jit(solution)/shard_map/increment/pallas_call | solution.py:300
  57.4 14.8 %all_to_all.21 = f32[16,48,128]{2,1,0:T(8,128)S(1)} all-to-all(f32[16,48,128]{2,1,0:T(8,128)S(1)} %bitcast.18), channel_id=1, replica_groups=mesh['mem'=16,'tile'=32] {'mem'}, dimensions={0} | all-to-all | bytes 786432 | tf_op jit(solution)/shard_map/all_to_all | solution.py:364
  72.2 18.1 %all_to_all.22 = f32[16,48,128]{2,1,0:T(8,128)S(1)} all-to-all(f32[16,48,128]{2,1,0:T(8,128)S(1)} %bitcast.20), channel_id=1, replica_groups=mesh['mem'=16,'tile'=32] {'mem'}, dimensions={0} | all-to-all | bytes 786432 | tf_op jit(solution)/shard_map/all_to_all | solution.py:364
  90.3 2.2 %project.3 = (f32[6,256,128]{2,1,0:T(8,128)S(1)}, f32[6,32,128]{2,1,0:T(8,128)S(1)}, f32[6,32,128]{2,1,0:T(8,128)S(1)}) custom-call(f32[24,3,2,8,16,128]{5,4,3,2,1,0:T(8,128)S(1)} %get-tuple-element.30.p_ref, f32[768,128]{1,0:T(8,128)S(1)} %bitcast.14, bf16[256,1024]{1,0:T(8,128)(2,1)S(1)} %get-tuple-element.32.m_ref), custom_call_target="tpu_custom_call" | custom-call | tf_op jit(solution)/shard_map/project/pallas_call | solution.py:194
  92.5 2.4 %collective-permute-start.4 = (f32[6,32,128]{2,1,0:T(8,128)S(1)}, f32[6,32,128]{2,1,0:T(8,128)S(1)}, u32[]{:S(2)}, u32[]{:S(2)}) collective-permute-start(f32[6,32,128]{2,1,0:T(8,128)S(1)} %get-tuple-element.48), channel_id=1, source_target_pairs={{0,1},{1,0},{2,3},{3,2},{4,5},{5,4},{6,7},{7,6},{8,9},{9,8},{10,11... | collective-permute-start | bytes 294920 | tf_op jit(solution)/shard_map/ppermute | solution.py:378
  94.9 1.9 %collective-permute-start.5 = (f32[6,32,128]{2,1,0:T(8,128)S(1)}, f32[6,32,128]{2,1,0:T(8,128)S(1)}, u32[]{:S(2)}, u32[]{:S(2)}) collective-permute-start(f32[6,32,128]{2,1,0:T(8,128)S(1)} %get-tuple-element.49), channel_id=1, source_target_pairs={{1,2},{2,1},{5,6},{6,5},{9,10},{10,9},{13,14},{14,13},{17,18},{18,... | collective-permute-start | bytes 294920 | tf_op jit(solution)/shard_map/ppermute | solution.py:377
  96.8 4.0 %collective-permute-done.5.far_ref = f32[6,32,128]{2,1,0:T(8,128)S(1)} collective-permute-done((f32[6,32,128]{2,1,0:T(8,128)S(1)}, f32[6,32,128]{2,1,0:T(8,128)S(1)}, u32[]{:S(2)}, u32[]{:S(2)}) %collective-permute-start.5) | collective-permute-done | bytes 98336 | tf_op jit(solution)/shard_map/ppermute | solution.py:377
  100.8 0.3 smooth_y.3
  101.1 1.9 %collective-permute-start.6 = (f32[6,32,128]{2,1,0:T(8,128)S(1)}, f32[6,32,128]{2,1,0:T(8,128)S(1)}, u32[]{:S(2)}, u32[]{:S(2)}) collective-permute-start(f32[6,32,128]{2,1,0:T(8,128)S(1)} %get-tuple-element.51), channel_id=1, source_target_pairs={{0,4},{1,5},{2,6},{3,7},{4,0},{5,1},{6,2},{7,3},{8,12},{9,13},{10,... | collective-permute-start | bytes 294920 | tf_op jit(solution)/shard_map/ppermute | solution.py:378
  103.1 10.0 %collective-permute-start.7 = (f32[6,32,128]{2,1,0:T(8,128)S(1)}, f32[6,32,128]{2,1,0:T(8,128)S(1)}, u32[]{:S(2)}, u32[]{:S(2)}) collective-permute-start(f32[6,32,128]{2,1,0:T(8,128)S(1)} %get-tuple-element.52), channel_id=1, source_target_pairs={{0,28},{1,29},{2,30},{3,31},{4,8},{5,9},{6,10},{7,11},{8,4},{9,5},... | collective-permute-start | bytes 294920 | tf_op jit(solution)/shard_map/ppermute | solution.py:377
  113.0 2.6 %collective-permute-done.7.far_ref = f32[6,32,128]{2,1,0:T(8,128)S(1)} collective-permute-done((f32[6,32,128]{2,1,0:T(8,128)S(1)}, f32[6,32,128]{2,1,0:T(8,128)S(1)}, u32[]{:S(2)}, u32[]{:S(2)}) %collective-permute-start.7) | collective-permute-done | bytes 98336 | tf_op jit(solution)/shard_map/ppermute | solution.py:377
  115.6 2.0 %increment.3 = f32[768,128]{1,0:T(8,128)S(1)} custom-call(f32[24,3,2,8,16,128]{5,4,3,2,1,0:T(8,128)S(1)} %get-tuple-element.30.p_ref, f32[6,256,128]{2,1,0:T(8,128)S(1)} %get-tuple-element.50.s_ref, f32[6,32,128]{2,1,0:T(8,128)S(1)} %collective-permute-done.6.near_ref, f32[6,32,128]{2,1,0:T(8,128)S(1)} %collective-permute-done.7.far_ref, ...), custom_call_target="tpu_custom_call" | custom-call | tf_op jit(solution)/shard_map/increment/pallas_call | solution.py:300
  117.7 14.5 %all_to_all.23 = f32[16,48,128]{2,1,0:T(8,128)S(1)} all-to-all(f32[16,48,128]{2,1,0:T(8,128)S(1)} %bitcast.17), channel_id=1, replica_groups=mesh['mem'=16,'tile'=32] {'mem'}, dimensions={0} | all-to-all | bytes 786432 | tf_op jit(solution)/shard_map/all_to_all | solution.py:364
  132.1 0.7 update.3
  (5 shorter events, 0.1 us)
Async XLA Ops:
  27.6 7.5 %collective-permute-start = (f32[6,32,128]{2,1,0:T(8,128)S(1)}, f32[6,32,128]{2,1,0:T(8,128)S(1)}, u32[]{:S(2)}, u32[]{:S(2)}) collective-permute-start(f32[6,32,128]{2,1,0:T(8,128)S(1)} %get-tuple-element.34), channel_id=1, source_target_pairs={{0,1},{1,0},{2,3},{3,2},{4,5},{5,4},{6,7},{7,6},{8,9},{9,8},{10,11... | collective-permute-start | bytes 294920 | tf_op jit(solution)/shard_map/ppermute | solution.py:378
  32.1 5.9 %collective-permute-start.1 = (f32[6,32,128]{2,1,0:T(8,128)S(1)}, f32[6,32,128]{2,1,0:T(8,128)S(1)}, u32[]{:S(2)}, u32[]{:S(2)}) collective-permute-start(f32[6,32,128]{2,1,0:T(8,128)S(1)} %get-tuple-element.35), channel_id=1, source_target_pairs={{1,2},{2,1},{5,6},{6,5},{9,10},{10,9},{13,14},{14,13},{17,18},{18,... | collective-permute-start | bytes 294920 | tf_op jit(solution)/shard_map/ppermute | solution.py:377
  38.4 14.4 %collective-permute-start.2 = (f32[6,32,128]{2,1,0:T(8,128)S(1)}, f32[6,32,128]{2,1,0:T(8,128)S(1)}, u32[]{:S(2)}, u32[]{:S(2)}) collective-permute-start(f32[6,32,128]{2,1,0:T(8,128)S(1)} %get-tuple-element.38), channel_id=1, source_target_pairs={{0,4},{1,5},{2,6},{3,7},{4,0},{5,1},{6,2},{7,3},{8,12},{9,13},{10,... | collective-permute-start | bytes 294920 | tf_op jit(solution)/shard_map/ppermute | solution.py:378
  43.0 12.3 %collective-permute-start.3 = (f32[6,32,128]{2,1,0:T(8,128)S(1)}, f32[6,32,128]{2,1,0:T(8,128)S(1)}, u32[]{:S(2)}, u32[]{:S(2)}) collective-permute-start(f32[6,32,128]{2,1,0:T(8,128)S(1)} %get-tuple-element.39), channel_id=1, source_target_pairs={{0,28},{1,29},{2,30},{3,31},{4,8},{5,9},{6,10},{7,11},{8,4},{9,5},... | collective-permute-start | bytes 294920 | tf_op jit(solution)/shard_map/ppermute | solution.py:377
  92.5 4.3 %collective-permute-start.4 = (f32[6,32,128]{2,1,0:T(8,128)S(1)}, f32[6,32,128]{2,1,0:T(8,128)S(1)}, u32[]{:S(2)}, u32[]{:S(2)}) collective-permute-start(f32[6,32,128]{2,1,0:T(8,128)S(1)} %get-tuple-element.48), channel_id=1, source_target_pairs={{0,1},{1,0},{2,3},{3,2},{4,5},{5,4},{6,7},{7,6},{8,9},{9,8},{10,11... | collective-permute-start | bytes 294920 | tf_op jit(solution)/shard_map/ppermute | solution.py:378
  94.9 5.9 %collective-permute-start.5 = (f32[6,32,128]{2,1,0:T(8,128)S(1)}, f32[6,32,128]{2,1,0:T(8,128)S(1)}, u32[]{:S(2)}, u32[]{:S(2)}) collective-permute-start(f32[6,32,128]{2,1,0:T(8,128)S(1)} %get-tuple-element.49), channel_id=1, source_target_pairs={{1,2},{2,1},{5,6},{6,5},{9,10},{10,9},{13,14},{14,13},{17,18},{18,... | collective-permute-start | bytes 294920 | tf_op jit(solution)/shard_map/ppermute | solution.py:377
  101.1 11.9 %collective-permute-start.6 = (f32[6,32,128]{2,1,0:T(8,128)S(1)}, f32[6,32,128]{2,1,0:T(8,128)S(1)}, u32[]{:S(2)}, u32[]{:S(2)}) collective-permute-start(f32[6,32,128]{2,1,0:T(8,128)S(1)} %get-tuple-element.51), channel_id=1, source_target_pairs={{0,4},{1,5},{2,6},{3,7},{4,0},{5,1},{6,2},{7,3},{8,12},{9,13},{10,... | collective-permute-start | bytes 294920 | tf_op jit(solution)/shard_map/ppermute | solution.py:378
  103.1 12.5 %collective-permute-start.7 = (f32[6,32,128]{2,1,0:T(8,128)S(1)}, f32[6,32,128]{2,1,0:T(8,128)S(1)}, u32[]{:S(2)}, u32[]{:S(2)}) collective-permute-start(f32[6,32,128]{2,1,0:T(8,128)S(1)} %get-tuple-element.52), channel_id=1, source_target_pairs={{0,28},{1,29},{2,30},{3,31},{4,8},{5,9},{6,10},{7,11},{8,4},{9,5},... | collective-permute-start | bytes 294920 | tf_op jit(solution)/shard_map/ppermute | solution.py:377

commit v3 on v2

--- a/solution.py
+++ b/solution.py
@@ -44,6 +44,13 @@
     return full.reshape(CELLS, COLS)
 
 
+def edge_matrix():
+    rows = interp_matrix().reshape(CY, CX, COLS)[:, [0, 1, CX - 2, CX - 1]]
+    rows = rows.transpose(1, 0, 2).reshape(4 * CY, CB, LANES)
+    blocks = [c for c in range(CB) if rows[:, c].any()]
+    return rows[:, blocks].reshape(4 * CY, -1), blocks
+
+
 def vmem():
     return pl.BlockSpec(memory_space=pltpu.VMEM)
 
@@ -73,8 +80,8 @@
 
 
 def opening_kernel(
-    p_ref, inn_ref, sv_ref, mask_ref, w_ref, kx_ref, ky_ref, mw_ref, m_ref,
-    split_ref, matrix_ref, innov_ref, static_ref, weight_ref, grad_ref, send_ref, cx_ref, cy_ref, scale_ref,
+    p_ref, inn_ref, sv_ref, mask_ref, w_ref, kx_ref, ky_ref, mw_ref, m_ref, ed_ref,
+    split_ref, matrix_ref, edge_ref, innov_ref, static_ref, weight_ref, grad_ref, send_ref, cx_ref, cy_ref, scale_ref,
     s_ref, *, size,
 ):
     own = inn_ref.shape[1]
@@ -108,6 +115,7 @@
         scale = jnp.dot(mw_ref[...], member, precision=exact, preferred_element_type=F32)
         scale_ref[...] = scale / float(size * members)
         matrix_ref[...] = m_ref[...]
+        edge_ref[...] = ed_ref[...]
 
     def one(k, carry):
         for v in range(VARS):
@@ -130,10 +138,12 @@
     small = [
         innovation, static_var, obs_mask.reshape(CB, LANES), obs_weight.T,
         kernel_x.T, kernel_y.T, member_weight.reshape(1, -1), jnp.asarray(interp_matrix(), BF16),
+        jnp.asarray(edge_matrix()[0], BF16),
     ]
     specs = [whole(x, pltpu.SMEM if n == 3 else pltpu.VMEM) for n, x in enumerate(small)]
     shapes = (
         [jax.ShapeDtypeStruct((members, VARS, own, CB, size, LANES), F32), jax.ShapeDtypeStruct((CELLS, COLS), BF16)]
+        + [jax.ShapeDtypeStruct(small[-1].shape, BF16)]
         + [jax.ShapeDtypeStruct((rows, LANES), F32)] * 4
         + [jax.ShapeDtypeStruct((size * rows, LANES), F32)]
         + [jax.ShapeDtypeStruct((5, own * LANES), F32)] * 2
@@ -256,8 +266,7 @@
     )(coarse, near, far, coefs)
 
 
-def increment_kernel(p_ref, s_ref, near_ref, far_ref, k_ref, w_ref, m_ref, o_ref, e_ref, hi_ref, lo_ref, f_ref, *, chunks):
-    odd_x = lax.axis_index("tile") // GRID_Y % 2 == 1
+def interior_kernel(p_ref, s_ref, k_ref, w_ref, m_ref, o_ref, e_ref, hi_ref, lo_ref, f_ref, *, chunks):
     members, _, _, _, owners, _ = p_ref.shape
     tiles = members * owners // LANES
     for n, q in enumerate(chunks):
@@ -265,10 +274,8 @@
             at = n * tiles + t
             for b in range(CY):
                 e_ref[at, b * EXT + 8 : b * EXT + 8 + CX, :] = s_ref[at, b * CX : (b + 1) * CX, :]
-            before, after = sides(near_ref[at], far_ref[at], odd_x)
-            for j in range(2):
-                e_ref[at, pl.ds(6 + j, CY, stride=EXT), :] = before[j * CY : (j + 1) * CY, :]
-                e_ref[at, pl.ds(8 + CX + j, CY, stride=EXT), :] = after[j * CY : (j + 1) * CY, :]
+            for j in (6, 7, 8 + CX, 9 + CX):
+                e_ref[at, pl.ds(j, CY, stride=EXT), :] = jnp.zeros((CY, LANES), F32)
             scale = w_ref[:, t * LANES : (t + 1) * LANES]
             coef = [k_ref[d : d + 1, q * LANES : (q + 1) * LANES] * scale for d in range(5)]
             for b in range(CY):
@@ -295,11 +302,11 @@
                 o_ref[pl.ds((n * VARS + v) * CB + c, owners, stride=len(chunks) * ROWS), :] = acc[v]
 
 
-def increment(split, smoothed, near, far, coefs, scale, matrix, chunks):
+def interior(split, smoothed, coefs, scale, matrix, chunks):
     members, _, _, _, owners, _ = split.shape
     return pl.pallas_call(
-        functools.partial(increment_kernel, chunks=chunks),
-        in_specs=[vmem()] * 7,
+        functools.partial(interior_kernel, chunks=chunks),
+        in_specs=[vmem()] * 5,
         out_specs=vmem(),
         out_shape=jax.ShapeDtypeStruct((owners * len(chunks) * ROWS, LANES), F32),
         scratch_shapes=[
@@ -309,8 +316,59 @@
             pltpu.VMEM((len(chunks), members * owners, COLS), F32),
         ],
         compiler_params=grant(8),
-        name="increment",
-    )(split, smoothed, near, far, coefs, scale, matrix)
+        name="interior",
+    )(split, smoothed, coefs, scale, matrix)
+
+
+def halo_kernel(p_ref, l_ref, near_ref, far_ref, k_ref, w_ref, m_ref, o_ref, hi_ref, lo_ref, f_ref, *, chunks, blocks):
+    odd_x = lax.axis_index("tile") // GRID_Y % 2 == 1
+    members, _, _, _, owners, _ = p_ref.shape
+    tiles = members * owners // LANES
+    stride = len(chunks) * ROWS
+    o_ref[...] = l_ref[...]
+    for n, q in enumerate(chunks):
+        for t in range(tiles):
+            before, after = sides(near_ref[n * tiles + t], far_ref[n * tiles + t], odd_x)
+            scale = w_ref[:, t * LANES : (t + 1) * LANES]
+            coef = [k_ref[d : d + 1, q * LANES : (q + 1) * LANES] * scale for d in range(5)]
+            cells = [
+                coef[0] * before[:CY] + coef[1] * before[CY:],
+                coef[0] * before[CY:],
+                coef[4] * after[:CY],
+                coef[3] * after[:CY] + coef[4] * after[CY:],
+            ]
+            for e, cell in enumerate(cells):
+                high, low = split_terms(cell)
+                hi_ref[n, e * CY : (e + 1) * CY, t * LANES : (t + 1) * LANES] = high
+                lo_ref[n, e * CY : (e + 1) * CY, t * LANES : (t + 1) * LANES] = low
+        dims = (((0,), (0,)), ((), ()))
+        fine = lax.dot_general(hi_ref[n], m_ref[...], dims, preferred_element_type=F32)
+        f_ref[n] = fine + lax.dot_general(lo_ref[n], m_ref[...], dims, preferred_element_type=F32)
+        for i, c in enumerate(blocks):
+            acc = [jnp.zeros((owners, LANES), F32)] * VARS
+            for k in range(members):
+                local = f_ref[n, k * owners : (k + 1) * owners, i * LANES : (i + 1) * LANES]
+                acc = [acc[v] + p_ref[k, v, q, c] * local for v in range(VARS)]
+            for v in range(VARS):
+                at = pl.ds((n * VARS + v) * CB + c, owners, stride=stride)
+                o_ref[at, :] = l_ref[at, :] + acc[v]
+
+
+def halo_part(split, partial, near, far, coefs, scale, edge, chunks):
+    members, _, _, _, owners, _ = split.shape
+    return pl.pallas_call(
+        functools.partial(halo_kernel, chunks=chunks, blocks=edge_matrix()[1]),
+        in_specs=[vmem()] * 7,
+        out_specs=vmem(),
+        out_shape=jax.ShapeDtypeStruct(partial.shape, F32),
+        scratch_shapes=[
+            pltpu.VMEM((len(chunks), edge.shape[0], members * owners), BF16),
+            pltpu.VMEM((len(chunks), edge.shape[0], members * owners), BF16),
+            pltpu.VMEM((len(chunks), members * owners, edge.shape[1]), F32),
+        ],
+        compiler_params=grant(6),
+        name="halo_part",
+    )(split, partial, near, far, coefs, scale, edge)
 
 
 def update_kernel(r_ref, *refs, size, last):
@@ -383,7 +441,7 @@
     size = lax.axis_size("mem")
     grid_x = lax.axis_size("tile") // GRID_Y
     chunks = tuple(range(perturbations.shape[2] // size))
-    split, matrix, innov, static, weight, gradient, to_send, coef_x, coef_y, scale = opening(
+    split, matrix, edge, innov, static, weight, gradient, to_send, coef_x, coef_y, scale = opening(
         perturbations, innovation, static_var, obs_mask, obs_weight, kernel_x, kernel_y, member_weight, size
     )
     analysis = None
@@ -393,7 +451,8 @@
         near, far = swapped(near, far, 1, GRID_Y, False)
         smoothed, near, far = smooth_y(coarse, near, far, coef_y, chunks)
         near, far = swapped(near, far, GRID_Y, grid_x, True)
-        partial = increment(split, smoothed, near, far, coef_x, scale, matrix, chunks)
+        partial = interior(split, smoothed, coef_x, scale, matrix, chunks)
+        partial = halo_part(split, partial, near, far, coef_x, scale, edge, chunks)
         received = exchange(partial, size)
         if step == STEPS - 1:
             return update(received, (analysis, gradient, static), size, True)[0]

time: 133 us -> 131 us (0.985)
  waiting for transfers between devices: 12 us -> 8.28 us
    ppermute x4, waiting for transfers between devices: 12 us -> 8.27 us  [swapped(): from_far = lax.ppermute(far, 'tile', pairs(False))]
    pallas_call x2 -> x4, Pallas kernels: 4.08 us -> 5.45 us  [the longest x2 3.75 us: interior(): pl.pallas_call(functools.partial(interior_kernel, chunks=chunks), in_spec...]
  transfers between devices with their start and end apart: 8 -> 8, of which waited for: 4 -> 4; matrix products, arithmetic and copies ran while one was open for 0% -> 0% of each run, Pallas kernels for 0% -> 3%
where the time goes in v3:
time: 131 us; the launch traced here: 130 us
  blocking collectives  67.7 us (52%)
  starting transfers between devices  38 us (29%)
  Pallas kernels  16.2 us (12%)
  waiting for transfers between devices  8.28 us (6%)
    all_to_all x4, blocking collectives, exchange(): return lax.all_to_all(blocks, 'mem', 0, 0, tiled=True).reshape(x.shape)  67.7 us
    ppermute x4, starting transfers between devices, swapped(): from_far = lax.ppermute(far, 'tile', pairs(False))  24.6 us
    ppermute x4, starting transfers between devices, swapped(): from_near = lax.ppermute(near, 'tile', pairs(True))  13.4 us
    ppermute x4, waiting for transfers between devices, swapped(): from_far = lax.ppermute(far, 'tile', pairs(False))  8.27 us
    pallas_call x1, Pallas kernels, opening(): pl.pallas_call(functools.partial(opening_kernel, size=size), grid=(member...  5.04 us
    pallas_call x2, Pallas kernels, project(): pl.pallas_call(functools.partial(project_kernel, chunks=chunks), in_specs...  4.42 us
    pallas_call x2, Pallas kernels, interior(): pl.pallas_call(functools.partial(interior_kernel, chunks=chunks), in_spec...  3.75 us
  transfers between devices with their start and end apart: 8, of which 4 were waited for; matrix products, arithmetic and copies ran while one was open for 0% of the time, Pallas kernels for 3%

profile of v3, /device:TPU:1, one launch (start us, length us, event | category | flops | bytes accessed | tf_op | source)
XLA Modules:
  0.0 130.3 jit_solution(15468305988066060781)
XLA Ops:
  0.0 5.0 %opening.1 = (f32[24,3,2,8,16,128]{5,4,3,2,1,0:T(8,128)S(1)}, bf16[256,1024]{1,0:T(8,128)(2,1)S(1)}, bf16[64,512]{1,0:T(8,128)(2,1)S(1)}, f32[48,128]{1,0:T(8,12...) custom-call(bf16[24,3,32,1024]{3,2,1,0:T(8,128)(2,1)} %p_ref.1, ...), custom_call_target="tpu_custom_call" | custom-call | tf_op jit(solution)/shard_map/opening/pallas_call | solution.py:152
  5.0 20.4 %all_to_all.20 = f32[16,48,128]{2,1,0:T(8,128)S(1)} all-to-all(f32[16,48,128]{2,1,0:T(8,128)S(1)} %bitcast.19), channel_id=1, replica_groups=mesh['mem'=16,'tile'=32] {'mem'}, dimensions={0} | all-to-all | bytes 786432 | tf_op jit(solution)/shard_map/all_to_all | solution.py:422
  25.4 2.2 %project.2 = (f32[6,256,128]{2,1,0:T(8,128)S(1)}, f32[6,32,128]{2,1,0:T(8,128)S(1)}, f32[6,32,128]{2,1,0:T(8,128)S(1)}) custom-call(f32[24,3,2,8,16,128]{5,4,3,2,1,0:T(8,128)S(1)} %get-tuple-element.31.p_ref, f32[768,128]{1,0:T(8,128)S(1)} %bitcast.14, bf16[256,1024]{1,0:T(8,128)(2,1)S(1)} %get-tuple-element.33.m_ref), custom_call_target="tpu_custom_call" | custom-call | tf_op jit(solution)/shard_map/project/pallas_call | solution.py:204
  27.6 4.4 %collective-permute-start = (f32[6,32,128]{2,1,0:T(8,128)S(1)}, f32[6,32,128]{2,1,0:T(8,128)S(1)}, u32[]{:S(2)}, u32[]{:S(2)}) collective-permute-start(f32[6,32,128]{2,1,0:T(8,128)S(1)} %get-tuple-element.35), channel_id=1, source_target_pairs={{0,1},{1,0},{2,3},{3,2},{4,5},{5,4},{6,7},{7,6},{8,9},{9,8},{10,11... | collective-permute-start | bytes 294920 | tf_op jit(solution)/shard_map/ppermute | solution.py:436
  32.1 3.0 %collective-permute-start.1 = (f32[6,32,128]{2,1,0:T(8,128)S(1)}, f32[6,32,128]{2,1,0:T(8,128)S(1)}, u32[]{:S(2)}, u32[]{:S(2)}) collective-permute-start(f32[6,32,128]{2,1,0:T(8,128)S(1)} %get-tuple-element.36), channel_id=1, source_target_pairs={{1,2},{2,1},{5,6},{6,5},{9,10},{10,9},{13,14},{14,13},{17,18},{18,... | collective-permute-start | bytes 294920 | tf_op jit(solution)/shard_map/ppermute | solution.py:435
  35.1 2.9 %collective-permute-done.1.far_ref = f32[6,32,128]{2,1,0:T(8,128)S(1)} collective-permute-done((f32[6,32,128]{2,1,0:T(8,128)S(1)}, f32[6,32,128]{2,1,0:T(8,128)S(1)}, u32[]{:S(2)}, u32[]{:S(2)}) %collective-permute-start.1) | collective-permute-done | bytes 98336 | tf_op jit(solution)/shard_map/ppermute | solution.py:435
  38.3 4.7 %collective-permute-start.2 = (f32[6,32,128]{2,1,0:T(8,128)S(1)}, f32[6,32,128]{2,1,0:T(8,128)S(1)}, u32[]{:S(2)}, u32[]{:S(2)}) collective-permute-start(f32[6,32,128]{2,1,0:T(8,128)S(1)} %get-tuple-element.41), channel_id=1, source_target_pairs={{0,4},{1,5},{2,6},{3,7},{4,0},{5,1},{6,2},{7,3},{8,12},{9,13},{10,... | collective-permute-start | bytes 294920 | tf_op jit(solution)/shard_map/ppermute | solution.py:436
  43.0 9.7 %collective-permute-start.3 = (f32[6,32,128]{2,1,0:T(8,128)S(1)}, f32[6,32,128]{2,1,0:T(8,128)S(1)}, u32[]{:S(2)}, u32[]{:S(2)}) collective-permute-start(f32[6,32,128]{2,1,0:T(8,128)S(1)} %get-tuple-element.42), channel_id=1, source_target_pairs={{0,28},{1,29},{2,30},{3,31},{4,8},{5,9},{6,10},{7,11},{8,4},{9,5},... | collective-permute-start | bytes 294920 | tf_op jit(solution)/shard_map/ppermute | solution.py:435
  52.7 1.9 %interior.2.l_ref = f32[768,128]{1,0:T(8,128)S(1)} custom-call(f32[24,3,2,8,16,128]{5,4,3,2,1,0:T(8,128)S(1)} %get-tuple-element.31.p_ref, f32[6,256,128]{2,1,0:T(8,128)S(1)} %get-tuple-element.38.s_ref, f32[5,256]{1,0:T(8,128)S(1)} %get-tuple-element.39.k_ref, f32[1,384]{1,0:T(1,128)S(1)} %get-tuple-element.40.w_ref, ...), custom_call_target="tpu_custom_call" | custom-call | tf_op jit(solution)/shard_map/interior/pallas_call | solution.py:307
  54.6 0.7 collective-permute-done.3.far_ref
  55.3 0.9 halo_part.2
  56.2 14.8 %all_to_all.21 = f32[16,48,128]{2,1,0:T(8,128)S(1)} all-to-all(f32[16,48,128]{2,1,0:T(8,128)S(1)} %bitcast.16), channel_id=1, replica_groups=mesh['mem'=16,'tile'=32] {'mem'}, dimensions={0} | all-to-all | bytes 786432 | tf_op jit(solution)/shard_map/all_to_all | solution.py:422
  71.0 18.1 %all_to_all.22 = f32[16,48,128]{2,1,0:T(8,128)S(1)} all-to-all(f32[16,48,128]{2,1,0:T(8,128)S(1)} %bitcast.20), channel_id=1, replica_groups=mesh['mem'=16,'tile'=32] {'mem'}, dimensions={0} | all-to-all | bytes 786432 | tf_op jit(solution)/shard_map/all_to_all | solution.py:422
  89.1 2.2 %project.3 = (f32[6,256,128]{2,1,0:T(8,128)S(1)}, f32[6,32,128]{2,1,0:T(8,128)S(1)}, f32[6,32,128]{2,1,0:T(8,128)S(1)}) custom-call(f32[24,3,2,8,16,128]{5,4,3,2,1,0:T(8,128)S(1)} %get-tuple-element.31.p_ref, f32[768,128]{1,0:T(8,128)S(1)} %bitcast.15, bf16[256,1024]{1,0:T(8,128)(2,1)S(1)} %get-tuple-element.33.m_ref), custom_call_target="tpu_custom_call" | custom-call | tf_op jit(solution)/shard_map/project/pallas_call | solution.py:204
  91.3 2.4 %collective-permute-start.4 = (f32[6,32,128]{2,1,0:T(8,128)S(1)}, f32[6,32,128]{2,1,0:T(8,128)S(1)}, u32[]{:S(2)}, u32[]{:S(2)}) collective-permute-start(f32[6,32,128]{2,1,0:T(8,128)S(1)} %get-tuple-element.50), channel_id=1, source_target_pairs={{0,1},{1,0},{2,3},{3,2},{4,5},{5,4},{6,7},{7,6},{8,9},{9,8},{10,11... | collective-permute-start | bytes 294920 | tf_op jit(solution)/shard_map/ppermute | solution.py:436
  93.7 1.9 %collective-permute-start.5 = (f32[6,32,128]{2,1,0:T(8,128)S(1)}, f32[6,32,128]{2,1,0:T(8,128)S(1)}, u32[]{:S(2)}, u32[]{:S(2)}) collective-permute-start(f32[6,32,128]{2,1,0:T(8,128)S(1)} %get-tuple-element.51), channel_id=1, source_target_pairs={{1,2},{2,1},{5,6},{6,5},{9,10},{10,9},{13,14},{14,13},{17,18},{18,... | collective-permute-start | bytes 294920 | tf_op jit(solution)/shard_map/ppermute | solution.py:435
  95.6 4.0 %collective-permute-done.5.far_ref = f32[6,32,128]{2,1,0:T(8,128)S(1)} collective-permute-done((f32[6,32,128]{2,1,0:T(8,128)S(1)}, f32[6,32,128]{2,1,0:T(8,128)S(1)}, u32[]{:S(2)}, u32[]{:S(2)}) %collective-permute-start.5) | collective-permute-done | bytes 98336 | tf_op jit(solution)/shard_map/ppermute | solution.py:435
  99.9 1.9 %collective-permute-start.6 = (f32[6,32,128]{2,1,0:T(8,128)S(1)}, f32[6,32,128]{2,1,0:T(8,128)S(1)}, u32[]{:S(2)}, u32[]{:S(2)}) collective-permute-start(f32[6,32,128]{2,1,0:T(8,128)S(1)} %get-tuple-element.53), channel_id=1, source_target_pairs={{0,4},{1,5},{2,6},{3,7},{4,0},{5,1},{6,2},{7,3},{8,12},{9,13},{10,... | collective-permute-start | bytes 294920 | tf_op jit(solution)/shard_map/ppermute | solution.py:436
  101.8 10.0 %collective-permute-start.7 = (f32[6,32,128]{2,1,0:T(8,128)S(1)}, f32[6,32,128]{2,1,0:T(8,128)S(1)}, u32[]{:S(2)}, u32[]{:S(2)}) collective-permute-start(f32[6,32,128]{2,1,0:T(8,128)S(1)} %get-tuple-element.54), channel_id=1, source_target_pairs={{0,28},{1,29},{2,30},{3,31},{4,8},{5,9},{6,10},{7,11},{8,4},{9,5},... | collective-permute-start | bytes 294920 | tf_op jit(solution)/shard_map/ppermute | solution.py:435
  111.8 1.9 %interior.3.l_ref = f32[768,128]{1,0:T(8,128)S(1)} custom-call(f32[24,3,2,8,16,128]{5,4,3,2,1,0:T(8,128)S(1)} %get-tuple-element.31.p_ref, f32[6,256,128]{2,1,0:T(8,128)S(1)} %get-tuple-element.52.s_ref, f32[5,256]{1,0:T(8,128)S(1)} %get-tuple-element.39.k_ref, f32[1,384]{1,0:T(1,128)S(1)} %get-tuple-element.40.w_ref, ...), custom_call_target="tpu_custom_call" | custom-call | tf_op jit(solution)/shard_map/interior/pallas_call | solution.py:307
  113.7 0.7 collective-permute-done.7.far_ref
  114.4 0.8 halo_part.3
  115.2 14.5 %all_to_all.23 = f32[16,48,128]{2,1,0:T(8,128)S(1)} all-to-all(f32[16,48,128]{2,1,0:T(8,128)S(1)} %bitcast.13), channel_id=1, replica_groups=mesh['mem'=16,'tile'=32] {'mem'}, dimensions={0} | all-to-all | bytes 786432 | tf_op jit(solution)/shard_map/all_to_all | solution.py:422
  129.7 0.7 update.3
  (7 shorter events, 0.7 us)
Async XLA Ops:
  27.6 7.5 %collective-permute-start = (f32[6,32,128]{2,1,0:T(8,128)S(1)}, f32[6,32,128]{2,1,0:T(8,128)S(1)}, u32[]{:S(2)}, u32[]{:S(2)}) collective-permute-start(f32[6,32,128]{2,1,0:T(8,128)S(1)} %get-tuple-element.35), channel_id=1, source_target_pairs={{0,1},{1,0},{2,3},{3,2},{4,5},{5,4},{6,7},{7,6},{8,9},{9,8},{10,11... | collective-permute-start | bytes 294920 | tf_op jit(solution)/shard_map/ppermute | solution.py:436
  32.1 5.9 %collective-permute-start.1 = (f32[6,32,128]{2,1,0:T(8,128)S(1)}, f32[6,32,128]{2,1,0:T(8,128)S(1)}, u32[]{:S(2)}, u32[]{:S(2)}) collective-permute-start(f32[6,32,128]{2,1,0:T(8,128)S(1)} %get-tuple-element.36), channel_id=1, source_target_pairs={{1,2},{2,1},{5,6},{6,5},{9,10},{10,9},{13,14},{14,13},{17,18},{18,... | collective-permute-start | bytes 294920 | tf_op jit(solution)/shard_map/ppermute | solution.py:435
  38.3 16.3 %collective-permute-start.2 = (f32[6,32,128]{2,1,0:T(8,128)S(1)}, f32[6,32,128]{2,1,0:T(8,128)S(1)}, u32[]{:S(2)}, u32[]{:S(2)}) collective-permute-start(f32[6,32,128]{2,1,0:T(8,128)S(1)} %get-tuple-element.41), channel_id=1, source_target_pairs={{0,4},{1,5},{2,6},{3,7},{4,0},{5,1},{6,2},{7,3},{8,12},{9,13},{10,... | collective-permute-start | bytes 294920 | tf_op jit(solution)/shard_map/ppermute | solution.py:436
  43.0 12.3 %collective-permute-start.3 = (f32[6,32,128]{2,1,0:T(8,128)S(1)}, f32[6,32,128]{2,1,0:T(8,128)S(1)}, u32[]{:S(2)}, u32[]{:S(2)}) collective-permute-start(f32[6,32,128]{2,1,0:T(8,128)S(1)} %get-tuple-element.42), channel_id=1, source_target_pairs={{0,28},{1,29},{2,30},{3,31},{4,8},{5,9},{6,10},{7,11},{8,4},{9,5},... | collective-permute-start | bytes 294920 | tf_op jit(solution)/shard_map/ppermute | solution.py:435
  91.3 4.3 %collective-permute-start.4 = (f32[6,32,128]{2,1,0:T(8,128)S(1)}, f32[6,32,128]{2,1,0:T(8,128)S(1)}, u32[]{:S(2)}, u32[]{:S(2)}) collective-permute-start(f32[6,32,128]{2,1,0:T(8,128)S(1)} %get-tuple-element.50), channel_id=1, source_target_pairs={{0,1},{1,0},{2,3},{3,2},{4,5},{5,4},{6,7},{7,6},{8,9},{9,8},{10,11... | collective-permute-start | bytes 294920 | tf_op jit(solution)/shard_map/ppermute | solution.py:436
  93.7 5.9 %collective-permute-start.5 = (f32[6,32,128]{2,1,0:T(8,128)S(1)}, f32[6,32,128]{2,1,0:T(8,128)S(1)}, u32[]{:S(2)}, u32[]{:S(2)}) collective-permute-start(f32[6,32,128]{2,1,0:T(8,128)S(1)} %get-tuple-element.51), channel_id=1, source_target_pairs={{1,2},{2,1},{5,6},{6,5},{9,10},{10,9},{13,14},{14,13},{17,18},{18,... | collective-permute-start | bytes 294920 | tf_op jit(solution)/shard_map/ppermute | solution.py:435
  99.9 13.8 %collective-permute-start.6 = (f32[6,32,128]{2,1,0:T(8,128)S(1)}, f32[6,32,128]{2,1,0:T(8,128)S(1)}, u32[]{:S(2)}, u32[]{:S(2)}) collective-permute-start(f32[6,32,128]{2,1,0:T(8,128)S(1)} %get-tuple-element.53), channel_id=1, source_target_pairs={{0,4},{1,5},{2,6},{3,7},{4,0},{5,1},{6,2},{7,3},{8,12},{9,13},{10,... | collective-permute-start | bytes 294920 | tf_op jit(solution)/shard_map/ppermute | solution.py:436
  101.8 12.5 %collective-permute-start.7 = (f32[6,32,128]{2,1,0:T(8,128)S(1)}, f32[6,32,128]{2,1,0:T(8,128)S(1)}, u32[]{:S(2)}, u32[]{:S(2)}) collective-permute-start(f32[6,32,128]{2,1,0:T(8,128)S(1)} %get-tuple-element.54), channel_id=1, source_target_pairs={{0,28},{1,29},{2,30},{3,31},{4,8},{5,9},{6,10},{7,11},{8,4},{9,5},... | collective-permute-start | bytes 294920 | tf_op jit(solution)/shard_map/ppermute | solution.py:435

commit v4 on v3

--- a/solution.py
+++ b/solution.py
@@ -82,7 +82,7 @@
 def opening_kernel(
     p_ref, inn_ref, sv_ref, mask_ref, w_ref, kx_ref, ky_ref, mw_ref, m_ref, ed_ref,
     split_ref, matrix_ref, edge_ref, innov_ref, static_ref, weight_ref, grad_ref, send_ref, cx_ref, cy_ref, scale_ref,
-    s_ref, *, size,
+    s_ref, *, size, steps,
 ):
     own = inn_ref.shape[1]
     shift = size.bit_length() - 1
@@ -90,15 +90,16 @@
     members = mw_ref.shape[1]
     start = pl.program_id(0) * block
 
-    @pl.when(pl.program_id(0) == 0)
+    def at_step(n):
+        return pl.when(pl.program_id(0) == min(n, steps - 1))
+
+    @at_step(0)
     def _():
         for q in range(own):
             for v in range(VARS):
                 for c in range(CB):
                     row = (q * VARS + v) * CB + c
-                    lanes = slice(c * LANES, (c + 1) * LANES)
-                    innov_ref[row : row + 1, :] = inn_ref[v, q : q + 1, lanes]
-                    static_ref[row : row + 1, :] = sv_ref[v, q : q + 1, lanes]
+                    innov_ref[row : row + 1, :] = inn_ref[v, q : q + 1, c * LANES : (c + 1) * LANES]
                 rows = slice((q * VARS + v) * CB, (q * VARS + v + 1) * CB)
                 weight_ref[rows, :] = mask_ref[...].astype(F32) * w_ref[q, v]
         grad = weight_ref[...] * (0.0 - innov_ref[...])
@@ -106,16 +107,34 @@
         rows = grad.shape[0]
         for d in range(size):
             send_ref[d * rows : (d + 1) * rows, :] = grad
+
+    @at_step(1)
+    def _():
         exact = lax.Precision.HIGHEST
         lane_bits = LANES.bit_length() - 1
         level = picked(levels, own * LANES, lambda c: own * (c & (size - 1)) + (c >> lane_bits))
-        member = picked(members, members * size, lambda c: c >> shift)
         cx_ref[...] = jnp.dot(kx_ref[...], level, precision=exact, preferred_element_type=F32)
         cy_ref[...] = jnp.dot(ky_ref[...], level, precision=exact, preferred_element_type=F32)
+
+    @at_step(2)
+    def _():
+        member = picked(members, members * size, lambda c: c >> shift)
+        exact = lax.Precision.HIGHEST
         scale = jnp.dot(mw_ref[...], member, precision=exact, preferred_element_type=F32)
         scale_ref[...] = scale / float(size * members)
+
+    @at_step(3)
+    def _():
         matrix_ref[...] = m_ref[...]
         edge_ref[...] = ed_ref[...]
+
+    @at_step(4)
+    def _():
+        for q in range(own):
+            for v in range(VARS):
+                for c in range(CB):
+                    row = (q * VARS + v) * CB + c
+                    static_ref[row : row + 1, :] = sv_ref[v, q : q + 1, c * LANES : (c + 1) * LANES]
 
     def one(k, carry):
         for v in range(VARS):
@@ -150,7 +169,7 @@
         + [jax.ShapeDtypeStruct((1, members * size), F32)]
     )
     return pl.pallas_call(
-        functools.partial(opening_kernel, size=size),
+        functools.partial(opening_kernel, size=size, steps=members // block),
         grid=(members // block,),
         in_specs=[pl.BlockSpec((block, VARS, levels, COLS), lambda k: (k, 0, 0, 0))] + specs,
         out_specs=[vmem()] * len(shapes),

time: 131 us -> 131 us (level)
  no operation moved by 1% of the time
where the time goes in v4:
time: 131 us; the launch traced here: 130 us
  blocking collectives  67.7 us (52%)
  starting transfers between devices  38 us (29%)
  Pallas kernels  16.3 us (12%)
  waiting for transfers between devices  8.29 us (6%)
    all_to_all x4, blocking collectives, exchange(): return lax.all_to_all(blocks, 'mem', 0, 0, tiled=True).reshape(x.shape)  67.7 us
    ppermute x4, starting transfers between devices, swapped(): from_far = lax.ppermute(far, 'tile', pairs(False))  24.6 us
    ppermute x4, starting transfers between devices, swapped(): from_near = lax.ppermute(near, 'tile', pairs(True))  13.4 us
    ppermute x4, waiting for transfers between devices, swapped(): from_far = lax.ppermute(far, 'tile', pairs(False))  8.28 us
    pallas_call x1, Pallas kernels, opening(): pl.pallas_call(functools.partial(opening_kernel, size=size, steps=members...  5.08 us
    pallas_call x2, Pallas kernels, project(): pl.pallas_call(functools.partial(project_kernel, chunks=chunks), in_specs...  4.41 us
    pallas_call x2, Pallas kernels, interior(): pl.pallas_call(functools.partial(interior_kernel, chunks=chunks), in_spec...  3.74 us
  transfers between devices with their start and end apart: 8, of which 4 were waited for; matrix products, arithmetic and copies ran while one was open for 0% of the time, Pallas kernels for 3%

profile of v4, /device:TPU:1, one launch (start us, length us, event | category | flops | bytes accessed | tf_op | source)
XLA Modules:
  0.0 130.4 jit_solution(12871615868930073805)
XLA Ops:
  0.0 5.1 %opening.1 = (f32[24,3,2,8,16,128]{5,4,3,2,1,0:T(8,128)S(1)}, bf16[256,1024]{1,0:T(8,128)(2,1)S(1)}, bf16[64,512]{1,0:T(8,128)(2,1)S(1)}, f32[48,128]{1,0:T(8,12...) custom-call(bf16[24,3,32,1024]{3,2,1,0:T(8,128)(2,1)} %p_ref.1, ...), custom_call_target="tpu_custom_call" | custom-call | tf_op jit(solution)/shard_map/opening/pallas_call | solution.py:171
  5.1 20.4 %all_to_all.20 = f32[16,48,128]{2,1,0:T(8,128)S(1)} all-to-all(f32[16,48,128]{2,1,0:T(8,128)S(1)} %bitcast.19), channel_id=1, replica_groups=mesh['mem'=16,'tile'=32] {'mem'}, dimensions={0} | all-to-all | bytes 786432 | tf_op jit(solution)/shard_map/all_to_all | solution.py:441
  25.5 2.2 %project.2 = (f32[6,256,128]{2,1,0:T(8,128)S(1)}, f32[6,32,128]{2,1,0:T(8,128)S(1)}, f32[6,32,128]{2,1,0:T(8,128)S(1)}) custom-call(f32[24,3,2,8,16,128]{5,4,3,2,1,0:T(8,128)S(1)} %get-tuple-element.31.p_ref, f32[768,128]{1,0:T(8,128)S(1)} %bitcast.14, bf16[256,1024]{1,0:T(8,128)(2,1)S(1)} %get-tuple-element.33.m_ref), custom_call_target="tpu_custom_call" | custom-call | tf_op jit(solution)/shard_map/project/pallas_call | solution.py:223
  27.7 4.5 %collective-permute-start = (f32[6,32,128]{2,1,0:T(8,128)S(1)}, f32[6,32,128]{2,1,0:T(8,128)S(1)}, u32[]{:S(2)}, u32[]{:S(2)}) collective-permute-start(f32[6,32,128]{2,1,0:T(8,128)S(1)} %get-tuple-element.35), channel_id=1, source_target_pairs={{0,1},{1,0},{2,3},{3,2},{4,5},{5,4},{6,7},{7,6},{8,9},{9,8},{10,11... | collective-permute-start | bytes 294920 | tf_op jit(solution)/shard_map/ppermute | solution.py:455
  32.1 3.0 %collective-permute-start.1 = (f32[6,32,128]{2,1,0:T(8,128)S(1)}, f32[6,32,128]{2,1,0:T(8,128)S(1)}, u32[]{:S(2)}, u32[]{:S(2)}) collective-permute-start(f32[6,32,128]{2,1,0:T(8,128)S(1)} %get-tuple-element.36), channel_id=1, source_target_pairs={{1,2},{2,1},{5,6},{6,5},{9,10},{10,9},{13,14},{14,13},{17,18},{18,... | collective-permute-start | bytes 294920 | tf_op jit(solution)/shard_map/ppermute | solution.py:454
  35.2 2.9 %collective-permute-done.1.far_ref = f32[6,32,128]{2,1,0:T(8,128)S(1)} collective-permute-done((f32[6,32,128]{2,1,0:T(8,128)S(1)}, f32[6,32,128]{2,1,0:T(8,128)S(1)}, u32[]{:S(2)}, u32[]{:S(2)}) %collective-permute-start.1) | collective-permute-done | bytes 98336 | tf_op jit(solution)/shard_map/ppermute | solution.py:454
  38.4 4.6 %collective-permute-start.2 = (f32[6,32,128]{2,1,0:T(8,128)S(1)}, f32[6,32,128]{2,1,0:T(8,128)S(1)}, u32[]{:S(2)}, u32[]{:S(2)}) collective-permute-start(f32[6,32,128]{2,1,0:T(8,128)S(1)} %get-tuple-element.41), channel_id=1, source_target_pairs={{0,4},{1,5},{2,6},{3,7},{4,0},{5,1},{6,2},{7,3},{8,12},{9,13},{10,... | collective-permute-start | bytes 294920 | tf_op jit(solution)/shard_map/ppermute | solution.py:455
  43.0 9.7 %collective-permute-start.3 = (f32[6,32,128]{2,1,0:T(8,128)S(1)}, f32[6,32,128]{2,1,0:T(8,128)S(1)}, u32[]{:S(2)}, u32[]{:S(2)}) collective-permute-start(f32[6,32,128]{2,1,0:T(8,128)S(1)} %get-tuple-element.42), channel_id=1, source_target_pairs={{0,28},{1,29},{2,30},{3,31},{4,8},{5,9},{6,10},{7,11},{8,4},{9,5},... | collective-permute-start | bytes 294920 | tf_op jit(solution)/shard_map/ppermute | solution.py:454
  52.8 1.9 %interior.2.l_ref = f32[768,128]{1,0:T(8,128)S(1)} custom-call(f32[24,3,2,8,16,128]{5,4,3,2,1,0:T(8,128)S(1)} %get-tuple-element.31.p_ref, f32[6,256,128]{2,1,0:T(8,128)S(1)} %get-tuple-element.38.s_ref, f32[5,256]{1,0:T(8,128)S(1)} %get-tuple-element.39.k_ref, f32[1,384]{1,0:T(1,128)S(1)} %get-tuple-element.40.w_ref, ...), custom_call_target="tpu_custom_call" | custom-call | tf_op jit(solution)/shard_map/interior/pallas_call | solution.py:326
  54.6 0.7 collective-permute-done.3.far_ref
  55.3 0.8 halo_part.2
  56.2 14.8 %all_to_all.21 = f32[16,48,128]{2,1,0:T(8,128)S(1)} all-to-all(f32[16,48,128]{2,1,0:T(8,128)S(1)} %bitcast.16), channel_id=1, replica_groups=mesh['mem'=16,'tile'=32] {'mem'}, dimensions={0} | all-to-all | bytes 786432 | tf_op jit(solution)/shard_map/all_to_all | solution.py:441
  71.1 18.1 %all_to_all.22 = f32[16,48,128]{2,1,0:T(8,128)S(1)} all-to-all(f32[16,48,128]{2,1,0:T(8,128)S(1)} %bitcast.20), channel_id=1, replica_groups=mesh['mem'=16,'tile'=32] {'mem'}, dimensions={0} | all-to-all | bytes 786432 | tf_op jit(solution)/shard_map/all_to_all | solution.py:441
  89.1 2.2 %project.3 = (f32[6,256,128]{2,1,0:T(8,128)S(1)}, f32[6,32,128]{2,1,0:T(8,128)S(1)}, f32[6,32,128]{2,1,0:T(8,128)S(1)}) custom-call(f32[24,3,2,8,16,128]{5,4,3,2,1,0:T(8,128)S(1)} %get-tuple-element.31.p_ref, f32[768,128]{1,0:T(8,128)S(1)} %bitcast.15, bf16[256,1024]{1,0:T(8,128)(2,1)S(1)} %get-tuple-element.33.m_ref), custom_call_target="tpu_custom_call" | custom-call | tf_op jit(solution)/shard_map/project/pallas_call | solution.py:223
  91.3 2.4 %collective-permute-start.4 = (f32[6,32,128]{2,1,0:T(8,128)S(1)}, f32[6,32,128]{2,1,0:T(8,128)S(1)}, u32[]{:S(2)}, u32[]{:S(2)}) collective-permute-start(f32[6,32,128]{2,1,0:T(8,128)S(1)} %get-tuple-element.50), channel_id=1, source_target_pairs={{0,1},{1,0},{2,3},{3,2},{4,5},{5,4},{6,7},{7,6},{8,9},{9,8},{10,11... | collective-permute-start | bytes 294920 | tf_op jit(solution)/shard_map/ppermute | solution.py:455
  93.7 1.9 %collective-permute-start.5 = (f32[6,32,128]{2,1,0:T(8,128)S(1)}, f32[6,32,128]{2,1,0:T(8,128)S(1)}, u32[]{:S(2)}, u32[]{:S(2)}) collective-permute-start(f32[6,32,128]{2,1,0:T(8,128)S(1)} %get-tuple-element.51), channel_id=1, source_target_pairs={{1,2},{2,1},{5,6},{6,5},{9,10},{10,9},{13,14},{14,13},{17,18},{18,... | collective-permute-start | bytes 294920 | tf_op jit(solution)/shard_map/ppermute | solution.py:454
  95.7 4.0 %collective-permute-done.5.far_ref = f32[6,32,128]{2,1,0:T(8,128)S(1)} collective-permute-done((f32[6,32,128]{2,1,0:T(8,128)S(1)}, f32[6,32,128]{2,1,0:T(8,128)S(1)}, u32[]{:S(2)}, u32[]{:S(2)}) %collective-permute-start.5) | collective-permute-done | bytes 98336 | tf_op jit(solution)/shard_map/ppermute | solution.py:454
  100.0 1.9 %collective-permute-start.6 = (f32[6,32,128]{2,1,0:T(8,128)S(1)}, f32[6,32,128]{2,1,0:T(8,128)S(1)}, u32[]{:S(2)}, u32[]{:S(2)}) collective-permute-start(f32[6,32,128]{2,1,0:T(8,128)S(1)} %get-tuple-element.53), channel_id=1, source_target_pairs={{0,4},{1,5},{2,6},{3,7},{4,0},{5,1},{6,2},{7,3},{8,12},{9,13},{10,... | collective-permute-start | bytes 294920 | tf_op jit(solution)/shard_map/ppermute | solution.py:455
  101.9 10.0 %collective-permute-start.7 = (f32[6,32,128]{2,1,0:T(8,128)S(1)}, f32[6,32,128]{2,1,0:T(8,128)S(1)}, u32[]{:S(2)}, u32[]{:S(2)}) collective-permute-start(f32[6,32,128]{2,1,0:T(8,128)S(1)} %get-tuple-element.54), channel_id=1, source_target_pairs={{0,28},{1,29},{2,30},{3,31},{4,8},{5,9},{6,10},{7,11},{8,4},{9,5},... | collective-permute-start | bytes 294920 | tf_op jit(solution)/shard_map/ppermute | solution.py:454
  111.8 1.9 %interior.3.l_ref = f32[768,128]{1,0:T(8,128)S(1)} custom-call(f32[24,3,2,8,16,128]{5,4,3,2,1,0:T(8,128)S(1)} %get-tuple-element.31.p_ref, f32[6,256,128]{2,1,0:T(8,128)S(1)} %get-tuple-element.52.s_ref, f32[5,256]{1,0:T(8,128)S(1)} %get-tuple-element.39.k_ref, f32[1,384]{1,0:T(1,128)S(1)} %get-tuple-element.40.w_ref, ...), custom_call_target="tpu_custom_call" | custom-call | tf_op jit(solution)/shard_map/interior/pallas_call | solution.py:326
  113.7 0.7 collective-permute-done.7.far_ref
  114.4 0.8 halo_part.3
  115.3 14.5 %all_to_all.23 = f32[16,48,128]{2,1,0:T(8,128)S(1)} all-to-all(f32[16,48,128]{2,1,0:T(8,128)S(1)} %bitcast.13), channel_id=1, replica_groups=mesh['mem'=16,'tile'=32] {'mem'}, dimensions={0} | all-to-all | bytes 786432 | tf_op jit(solution)/shard_map/all_to_all | solution.py:441
  129.7 0.7 update.3
  (7 shorter events, 0.7 us)
Async XLA Ops:
  27.7 7.5 %collective-permute-start = (f32[6,32,128]{2,1,0:T(8,128)S(1)}, f32[6,32,128]{2,1,0:T(8,128)S(1)}, u32[]{:S(2)}, u32[]{:S(2)}) collective-permute-start(f32[6,32,128]{2,1,0:T(8,128)S(1)} %get-tuple-element.35), channel_id=1, source_target_pairs={{0,1},{1,0},{2,3},{3,2},{4,5},{5,4},{6,7},{7,6},{8,9},{9,8},{10,11... | collective-permute-start | bytes 294920 | tf_op jit(solution)/shard_map/ppermute | solution.py:455
  32.1 5.9 %collective-permute-start.1 = (f32[6,32,128]{2,1,0:T(8,128)S(1)}, f32[6,32,128]{2,1,0:T(8,128)S(1)}, u32[]{:S(2)}, u32[]{:S(2)}) collective-permute-start(f32[6,32,128]{2,1,0:T(8,128)S(1)} %get-tuple-element.36), channel_id=1, source_target_pairs={{1,2},{2,1},{5,6},{6,5},{9,10},{10,9},{13,14},{14,13},{17,18},{18,... | collective-permute-start | bytes 294920 | tf_op jit(solution)/shard_map/ppermute | solution.py:454
  38.4 16.2 %collective-permute-start.2 = (f32[6,32,128]{2,1,0:T(8,128)S(1)}, f32[6,32,128]{2,1,0:T(8,128)S(1)}, u32[]{:S(2)}, u32[]{:S(2)}) collective-permute-start(f32[6,32,128]{2,1,0:T(8,128)S(1)} %get-tuple-element.41), channel_id=1, source_target_pairs={{0,4},{1,5},{2,6},{3,7},{4,0},{5,1},{6,2},{7,3},{8,12},{9,13},{10,... | collective-permute-start | bytes 294920 | tf_op jit(solution)/shard_map/ppermute | solution.py:455
  43.0 12.3 %collective-permute-start.3 = (f32[6,32,128]{2,1,0:T(8,128)S(1)}, f32[6,32,128]{2,1,0:T(8,128)S(1)}, u32[]{:S(2)}, u32[]{:S(2)}) collective-permute-start(f32[6,32,128]{2,1,0:T(8,128)S(1)} %get-tuple-element.42), channel_id=1, source_target_pairs={{0,28},{1,29},{2,30},{3,31},{4,8},{5,9},{6,10},{7,11},{8,4},{9,5},... | collective-permute-start | bytes 294920 | tf_op jit(solution)/shard_map/ppermute | solution.py:454
  91.3 4.3 %collective-permute-start.4 = (f32[6,32,128]{2,1,0:T(8,128)S(1)}, f32[6,32,128]{2,1,0:T(8,128)S(1)}, u32[]{:S(2)}, u32[]{:S(2)}) collective-permute-start(f32[6,32,128]{2,1,0:T(8,128)S(1)} %get-tuple-element.50), channel_id=1, source_target_pairs={{0,1},{1,0},{2,3},{3,2},{4,5},{5,4},{6,7},{7,6},{8,9},{9,8},{10,11... | collective-permute-start | bytes 294920 | tf_op jit(solution)/shard_map/ppermute | solution.py:455
  93.7 5.9 %collective-permute-start.5 = (f32[6,32,128]{2,1,0:T(8,128)S(1)}, f32[6,32,128]{2,1,0:T(8,128)S(1)}, u32[]{:S(2)}, u32[]{:S(2)}) collective-permute-start(f32[6,32,128]{2,1,0:T(8,128)S(1)} %get-tuple-element.51), channel_id=1, source_target_pairs={{1,2},{2,1},{5,6},{6,5},{9,10},{10,9},{13,14},{14,13},{17,18},{18,... | collective-permute-start | bytes 294920 | tf_op jit(solution)/shard_map/ppermute | solution.py:454
  100.0 13.8 %collective-permute-start.6 = (f32[6,32,128]{2,1,0:T(8,128)S(1)}, f32[6,32,128]{2,1,0:T(8,128)S(1)}, u32[]{:S(2)}, u32[]{:S(2)}) collective-permute-start(f32[6,32,128]{2,1,0:T(8,128)S(1)} %get-tuple-element.53), channel_id=1, source_target_pairs={{0,4},{1,5},{2,6},{3,7},{4,0},{5,1},{6,2},{7,3},{8,12},{9,13},{10,... | collective-permute-start | bytes 294920 | tf_op jit(solution)/shard_map/ppermute | solution.py:455
  101.9 12.5 %collective-permute-start.7 = (f32[6,32,128]{2,1,0:T(8,128)S(1)}, f32[6,32,128]{2,1,0:T(8,128)S(1)}, u32[]{:S(2)}, u32[]{:S(2)}) collective-permute-start(f32[6,32,128]{2,1,0:T(8,128)S(1)} %get-tuple-element.54), channel_id=1, source_target_pairs={{0,28},{1,29},{2,30},{3,31},{4,8},{5,9},{6,10},{7,11},{8,4},{9,5},... | collective-permute-start | bytes 294920 | tf_op jit(solution)/shard_map/ppermute | solution.py:454
